TPU v7x, 512 devices: a whole 4x4x16 slice. The times are simulated.
512 devices in a mesh: dom: 8 (over z_lo), col: 8 (over y, core), rep: 8 (over z_hi, x).
Axes of the slice: x: 4, y: 4, z: 16 (z_hi: 2, z_lo: 8; z = z_hi * 8 + z_lo), core: 2. Of those that a mesh axis runs over, the one named last changes fastest.
Arguments:
- features: bfloat16 [8, 8192, 100], P('rep', 'dom'), may hold values from -6 to 6
- w_in: bfloat16 [100, 256], P(None, 'col'), may hold values from -0.625 to 0.625
- w_hidden: bfloat16 [256, 256], P('col'), may hold values from -0.375 to 0.375
- blocks: bfloat16 [8, 8, 8, 512, 512], P('rep', 'dom'), may hold values from -0.125 to 0.125
- block_list: int32 [8, 8, 8, 3], P('rep', 'dom'), may hold values from 0 to 7, as said below
- block_count: int32 [8, 8], P('rep', 'dom'), may hold values from 1 to 8, as said below
- cotangent: bfloat16 [8, 8192, 256], P('rep', 'dom', 'col'), may hold values from -6 to 6
Outputs:
- out_hidden: bfloat16 [8, 8192, 256], P('rep', 'dom', 'col')
- grad_hidden: float32 [256, 256], P('col', ('dom', 'rep'))
Inputs may be any that keep to these rules, and one draw needn't show every extreme that they name: `block_list`: each slot holds a row cluster below 2, a partner partition below 8 and a partner cluster below 2; the same cluster pair may stand in several slots, and then their blocks add. `block_count`: in every batch some partition uses all 8 slots.
All inputs are finite; a program needn't handle non-finite values.
Results may differ from a plain program's by a relative error of at most 0.0065.
Values may be sent and summed in bfloat16 or wider, within the bound.
A program may use at most 64 MiB of HBM per device.

v0:
```python
import jax
import jax.numpy as jnp
from jax import lax
from jax.sharding import Mesh
from jax.sharding import PartitionSpec as P

COL = ("col_0", "col_1")


def laid_out(tiles, dim):
    lengths = list(tiles.shape[1:])
    lengths[dim] *= tiles.shape[0]
    return jnp.moveaxis(tiles, 0, dim).reshape(lengths)


def sent_to_all(x, axis):
    copies = jnp.broadcast_to(x, (lax.axis_size(axis), *x.shape))
    return lax.all_to_all(copies, axis, split_axis=0, concat_axis=0, tiled=True)


def gathered_copies(x, axis, dim):
    return laid_out(sent_to_all(x, axis), dim)


def whole_of(x, axes, dim):
    for axis in reversed(axes):
        x = lax.all_gather(x, axis, axis=dim, tiled=True)
    return x


def in_blocks(x, dim, devices):
    lengths = x.shape
    tiles = x.reshape(*lengths[:dim], devices, lengths[dim] // devices, *lengths[dim + 1 :])
    return jnp.moveaxis(tiles, dim, 0)


def summed_on_arrival(x, axis, dim):
    tiles = in_blocks(x, dim, lax.axis_size(axis))
    arrived = lax.all_to_all(tiles, axis, split_axis=0, concat_axis=0, tiled=True)
    return arrived.sum(axis=0)


def body(features, w_in, w_hidden, blocks, block_list, block_count, cotangent):
    rows = features.shape[1]
    slots = blocks.shape[2]
    clus = blocks.shape[3]
    width = w_in.shape[1]
    local_blocks = blocks[0, 0]
    lists = block_list[0, 0]
    count = block_count[0, 0]
    target = lists[:, 0] * clus
    source = lists[:, 1] * rows + lists[:, 2] * clus

    def fold_slabs(acc, piece):
        length = piece.shape[0]
        for slot in range(slots):
            offset = source[slot]
            valid = (slot < count) & (offset >= 0) & (offset < length)

            def fold_apply(total, slot=slot, offset=offset):
                part = lax.dynamic_slice_in_dim(piece, offset, clus, 0)
                term = jnp.dot(local_blocks[slot], part, preferred_element_type=jnp.float32)
                current = lax.dynamic_slice_in_dim(total, target[slot], clus, 0)
                return lax.dynamic_update_slice_in_dim(total, current + term, target[slot], 0)

            acc = lax.cond(valid, fold_apply, lambda total: total, acc)
        return acc

    empty = jnp.zeros((rows, width), jnp.float32)
    z1 = jnp.dot(features[0], w_in, preferred_element_type=jnp.float32).astype(jnp.bfloat16)
    p1 = fold_slabs(empty, gathered_copies(z1, "dom", 0))
    h1 = jax.nn.gelu(p1, approximate=True).astype(jnp.bfloat16)
    full_weight = gathered_copies(w_hidden, COL, 0)
    weight_rows = lax.dynamic_slice_in_dim(full_weight, lax.axis_index(COL) * width, width, 1)
    all_hidden = whole_of(h1, COL, 1)
    z2 = jnp.dot(all_hidden, weight_rows, preferred_element_type=jnp.float32).astype(jnp.bfloat16)
    p2 = fold_slabs(empty, gathered_copies(z2, "dom", 0))
    upstream = cotangent[0]
    term_rows = jnp.zeros((rows * lax.axis_size("dom"), width), jnp.float32)
    for slot in range(slots):
        offset = source[slot]
        valid = (slot < count) & (offset >= 0) & (offset < rows * lax.axis_size("dom"))

        def spread_apply(total, slot=slot, offset=offset):
            part = lax.dynamic_slice_in_dim(upstream, target[slot], clus, 0)
            term = lax.dot_general(
                local_blocks[slot],
                part,
                (((0,), (0,)), ((), ())),
                preferred_element_type=jnp.float32,
            )
            current = lax.dynamic_slice_in_dim(total, offset, clus, 0)
            return lax.dynamic_update_slice_in_dim(total, current + term, offset, 0)

        term_rows = lax.cond(valid, spread_apply, lambda total: total, term_rows)
    dz2 = summed_on_arrival(term_rows, "dom", 0).astype(jnp.bfloat16)
    local_grad = lax.dot_general(
        h1,
        gathered_copies(dz2, COL, 1),
        (((0,), (0,)), ((), ())),
        preferred_element_type=jnp.float32,
    )
    grad = summed_on_arrival(local_grad, ("dom", "rep"), 1)
    return (p2.astype(jnp.bfloat16)[None], grad)


def solution(mesh):
    torus = Mesh(
        mesh.devices.reshape(mesh.shape["dom"], 4, 2, mesh.shape["rep"]),
        ("dom", "col_0", "col_1", "rep"),
    )
    placed = (
        P("rep", "dom", None),
        P(None, COL),
        P(COL, None),
        P("rep", "dom", None, None, None),
        P("rep", "dom", None, None),
        P("rep", "dom"),
        P("rep", "dom", COL),
    )
    return jax.shard_map(
        body,
        mesh=torus,
        in_specs=placed,
        out_specs=(P("rep", "dom", COL), P(COL, ("dom", "rep"))),
        check_vma=False,
    )
```

profile of v0, /device:TPU:24, one launch (start us, length us, event | category | flops | bytes accessed | tf_op | source)
XLA Modules:
  0.0 328.7 jit_solution(5366484160664684083)
XLA Ops:
  2.1 8.9 %all-to-all-start.1 = ((bf16[8,32,256]{2,1,0:T(8,128)(2,1)}), bf16[8,32,256]{2,1,0:T(8,128)(2,1)S(1)}, u32[]{:S(2)}, u32[]{:S(2)}) async-start(bf16[8,32,256]{2,1,0:T(8,128)(2,1)} %broadcast_in_dim.40), calls=%async_computation.1 | async-start | bytes 262144 | tf_op jit(solution)/shard_map/all_to_all | solution.py:18
  15.8 8.4 %all-to-all-start = ((bf16[8,1024,32]{1,2,0:T(8,128)(2,1)}), bf16[8,1024,32]{1,2,0:T(8,128)(2,1)S(1)}, u32[]{:S(2)}, u32[]{:S(2)}) async-start(bf16[8,1024,32]{1,2,0:T(8,128)(2,1)} %broadcast_in_dim.39), calls=%async_computation | async-start | bytes 1048576 | tf_op jit(solution)/shard_map/all_to_all | solution.py:18
  37.2 5.9 %conditional.40 = (f32[8192,32]{0,1:T(8,128)}) conditional(s32[]{:T(128)} %convert_element_type.68, () %tuple.190, (s32[8]{0:T(128)S(1)}, bf16[1024,32]{1,0:T(8,128)(2,1)S(1)}, bf16[8,512,512]{2,1,0:T(8,128)(2,1)}, s32[]{:T(128)}) %tuple.312), branch_computations={%region_32.0_spmd, %region_33.0_spmd} | conditional | flops 16777220 | bytes 1900632 | solution.py:95
  43.2 7.1 %conditional.41 = (f32[8192,32]{0,1:T(8,128)}) conditional(s32[]{:T(128)} %convert_element_type.67, f32[8192,32]{0,1:T(8,128)} %get-tuple-element.562, (s32[]{:T(128)}, f32[8192,32]{0,1:T(8,128)}, s32[8]{0:T(128)S(1)}, bf16[1024,32]{1,0:T(8,128)(2,1)S(1)}, bf16[8,512,512]{2,1,0:T(8,128)(2,1)}) %tuple.313), branch_computations={%region_34.0_spmd, %region_35.0_spmd} | conditional | flops 16793606 | bytes 917600 | solution.py:95
  50.3 7.1 %conditional.42 = (f32[8192,32]{0,1:T(8,128)}) conditional(s32[]{:T(128)} %convert_element_type.66, f32[8192,32]{0,1:T(8,128)} %get-tuple-element.563, (s32[]{:T(128)}, f32[8192,32]{0,1:T(8,128)}, s32[8]{0:T(128)S(1)}, bf16[1024,32]{1,0:T(8,128)(2,1)S(1)}, bf16[8,512,512]{2,1,0:T(8,128)(2,1)}) %tuple.314), branch_computations={%region_36.0_spmd, %region_37.0_spmd} | conditional | flops 16793606 | bytes 917600 | solution.py:95
  57.4 7.3 %conditional.43 = (f32[8192,32]{0,1:T(8,128)}) conditional(s32[]{:T(128)} %convert_element_type.65, f32[8192,32]{0,1:T(8,128)} %get-tuple-element.564, (s32[]{:T(128)}, f32[8192,32]{0,1:T(8,128)}, s32[8]{0:T(128)S(1)}, bf16[1024,32]{1,0:T(8,128)(2,1)S(1)}, bf16[8,512,512]{2,1,0:T(8,128)(2,1)}) %tuple.315), branch_computations={%region_38.0_spmd, %region_39.0_spmd} | conditional | flops 16793606 | bytes 917600 | solution.py:95
  64.8 7.0 %conditional.44 = (f32[8192,32]{0,1:T(8,128)}) conditional(s32[]{:T(128)} %convert_element_type.64, f32[8192,32]{0,1:T(8,128)} %get-tuple-element.565, (s32[]{:T(128)}, f32[8192,32]{0,1:T(8,128)}, s32[8]{0:T(128)S(1)}, bf16[1024,32]{1,0:T(8,128)(2,1)S(1)}, bf16[8,512,512]{2,1,0:T(8,128)(2,1)}) %tuple.316), branch_computations={%region_40.0_spmd, %region_41.0_spmd} | conditional | flops 16793606 | bytes 917600 | solution.py:95
  74.1 26.6 %all-to-all-start.3 = ((f32[8,1024,32]{1,2,0:T(8,128)}), f32[8,1024,32]{1,2,0:T(8,128)S(1)}, u32[]{:S(2)}, u32[]{:S(2)}) async-start(f32[8,1024,32]{1,2,0:T(8,128)} %bitcast.236), calls=%async_computation.3 | async-start | bytes 2097152 | tf_op jit(solution)/shard_map/all_to_all | solution.py:39
  100.7 7.4 %conditional.24 = (f32[1024,32]{0,1:T(8,128)}) conditional(s32[]{:T(128)} %convert_element_type.68, () %tuple.173, (s32[]{:T(128)}, bf16[8192,32]{0,1:T(8,128)(2,1)S(1)}, bf16[8,512,512]{2,1,0:T(8,128)(2,1)}, s32[8]{0:T(128)S(1)}) %tuple.296), branch_computations={%region_0.0_spmd, %region_1.0_spmd} | conditional | flops 16777220 | bytes 2031704 | solution.py:66
  108.1 9.3 %conditional.25 = (f32[1024,32]{0,1:T(8,128)}) conditional(s32[]{:T(128)} %convert_element_type.67, f32[1024,32]{0,1:T(8,128)} %get-tuple-element.546, (s32[8]{0:T(128)S(1)}, f32[1024,32]{0,1:T(8,128)}, s32[]{:T(128)}, bf16[8192,32]{0,1:T(8,128)(2,1)S(1)}, bf16[8,512,512]{2,1,0:T(8,128)(2,1)}) %tuple.297), branch_computations={%region_2.0_spmd, %region_3.0_spmd} | conditional | flops 16793606 | bytes 1966176 | solution.py:66
  117.3 9.2 %conditional.26 = (f32[1024,32]{0,1:T(8,128)}) conditional(s32[]{:T(128)} %convert_element_type.66, f32[1024,32]{0,1:T(8,128)} %get-tuple-element.547, (s32[8]{0:T(128)S(1)}, f32[1024,32]{0,1:T(8,128)}, s32[]{:T(128)}, bf16[8192,32]{0,1:T(8,128)(2,1)S(1)}, bf16[8,512,512]{2,1,0:T(8,128)(2,1)}) %tuple.298), branch_computations={%region_4.0_spmd, %region_5.0_spmd} | conditional | flops 16793606 | bytes 1966176 | solution.py:66
  126.5 9.5 %conditional.27 = (f32[1024,32]{0,1:T(8,128)}) conditional(s32[]{:T(128)} %convert_element_type.65, f32[1024,32]{0,1:T(8,128)} %get-tuple-element.548, (s32[8]{0:T(128)S(1)}, f32[1024,32]{0,1:T(8,128)}, s32[]{:T(128)}, bf16[8192,32]{0,1:T(8,128)(2,1)S(1)}, bf16[8,512,512]{2,1,0:T(8,128)(2,1)}) %tuple.299), branch_computations={%region_6.0_spmd, %region_7.0_spmd} | conditional | flops 16793606 | bytes 1966176 | solution.py:66
  136.0 9.1 %conditional.28 = (f32[1024,32]{0,1:T(8,128)}) conditional(s32[]{:T(128)} %convert_element_type.64, f32[1024,32]{0,1:T(8,128)} %get-tuple-element.549, (s32[8]{0:T(128)S(1)}, f32[1024,32]{0,1:T(8,128)}, s32[]{:T(128)}, bf16[8192,32]{0,1:T(8,128)(2,1)S(1)}, bf16[8,512,512]{2,1,0:T(8,128)(2,1)}) %tuple.300), branch_computations={%region_8.0_spmd, %region_9.0_spmd} | conditional | flops 16793606 | bytes 1966176 | solution.py:66
  148.0 12.8 %all_gather.7 = bf16[1024,256]{0,1:T(8,128)(2,1)S(1)} all-gather(bf16[1024,64]{0,1:T(8,128)(2,1)S(1)} %all_gather.6), channel_id=1, replica_groups=mesh['dom'=8,'col_0'=4,'col_1'=2,'rep'=8] {'col_0'}, dimensions={1}, use_global_device_ids=true | all-gather | bytes 655360 | tf_op jit(solution)/shard_map/all_gather | solution.py:27
  161.9 32.8 %all-to-all-start.2 = ((bf16[8,1024,32]{1,2,0:T(8,128)(2,1)}), bf16[8,1024,32]{1,2,0:T(8,128)(2,1)S(1)}, u32[]{:S(2)}, u32[]{:S(2)}) async-start(bf16[8,1024,32]{1,2,0:T(8,128)(2,1)} %broadcast_in_dim.41), calls=%async_computation.2 | async-start | bytes 1048576 | tf_op jit(solution)/shard_map/all_to_all | solution.py:18
  194.8 26.5 %all-to-all-done.2 = bf16[8,1024,32]{1,2,0:T(8,128)(2,1)S(1)} async-done(((bf16[8,1024,32]{1,2,0:T(8,128)(2,1)}), bf16[8,1024,32]{1,2,0:T(8,128)(2,1)S(1)}, u32[]{:S(2)}, u32[]{:S(2)}) %all-to-all-start.2) | async-done | bytes 524320 | tf_op jit(solution)/shard_map/all_to_all | solution.py:18
  222.1 5.1 %all-to-all-start.4 = ((bf16[8,1024,32]{1,2,0:T(8,128)(2,1)}), bf16[8,1024,32]{1,2,0:T(8,128)(2,1)S(1)}, u32[]{:S(2)}, u32[]{:S(2)}) async-start(bf16[8,1024,32]{1,2,0:T(8,128)(2,1)} %broadcast_in_dim.43), calls=%async_computation.4 | async-start | bytes 1048576 | tf_op jit(solution)/shard_map/all_to_all | solution.py:18
  227.3 6.6 %conditional.32 = (f32[1024,32]{0,1:T(8,128)}) conditional(s32[]{:T(128)} %convert_element_type.68, () %tuple.172, (s32[]{:T(128)}, bf16[8192,32]{0,1:T(8,128)(2,1)S(1)}, bf16[8,512,512]{2,1,0:T(8,128)(2,1)}, s32[8]{0:T(128)S(1)}) %tuple.304), branch_computations={%region_16.0_spmd, %region_17.0_spmd} | conditional | flops 16777220 | bytes 2031704 | solution.py:66
  233.8 8.3 %conditional.33 = (f32[1024,32]{0,1:T(8,128)}) conditional(s32[]{:T(128)} %convert_element_type.67, f32[1024,32]{0,1:T(8,128)} %get-tuple-element.554, (s32[8]{0:T(128)S(1)}, f32[1024,32]{0,1:T(8,128)}, s32[]{:T(128)}, bf16[8192,32]{0,1:T(8,128)(2,1)S(1)}, bf16[8,512,512]{2,1,0:T(8,128)(2,1)}) %tuple.305), branch_computations={%region_18.0_spmd, %region_19.0_spmd} | conditional | flops 16793606 | bytes 1966176 | solution.py:66
  242.1 8.2 %conditional.34 = (f32[1024,32]{0,1:T(8,128)}) conditional(s32[]{:T(128)} %convert_element_type.66, f32[1024,32]{0,1:T(8,128)} %get-tuple-element.555, (s32[8]{0:T(128)S(1)}, f32[1024,32]{0,1:T(8,128)}, s32[]{:T(128)}, bf16[8192,32]{0,1:T(8,128)(2,1)S(1)}, bf16[8,512,512]{2,1,0:T(8,128)(2,1)}) %tuple.306), branch_computations={%region_20.0_spmd, %region_21.0_spmd} | conditional | flops 16793606 | bytes 1966176 | solution.py:66
  250.3 8.5 %conditional.35 = (f32[1024,32]{0,1:T(8,128)}) conditional(s32[]{:T(128)} %convert_element_type.65, f32[1024,32]{0,1:T(8,128)} %get-tuple-element.556, (s32[8]{0:T(128)S(1)}, f32[1024,32]{0,1:T(8,128)}, s32[]{:T(128)}, bf16[8192,32]{0,1:T(8,128)(2,1)S(1)}, bf16[8,512,512]{2,1,0:T(8,128)(2,1)}) %tuple.307), branch_computations={%region_22.0_spmd, %region_23.0_spmd} | conditional | flops 16793606 | bytes 1966176 | solution.py:66
  258.8 8.1 %conditional.36 = (f32[1024,32]{0,1:T(8,128)}) conditional(s32[]{:T(128)} %convert_element_type.64, f32[1024,32]{0,1:T(8,128)} %get-tuple-element.557, (s32[8]{0:T(128)S(1)}, f32[1024,32]{0,1:T(8,128)}, s32[]{:T(128)}, bf16[8192,32]{0,1:T(8,128)(2,1)S(1)}, bf16[8,512,512]{2,1,0:T(8,128)(2,1)}) %tuple.308), branch_computations={%region_24.0_spmd, %region_25.0_spmd} | conditional | flops 16793606 | bytes 1966176 | solution.py:66
  268.3 44.3 %all-to-all-start.5 = ((f32[64,1,128]{2,1,0:T(1,128)}), f32[64,1,128]{2,1,0:T(1,128)S(1)}, u32[]{:S(2)}, u32[]{:S(2)}) async-start(f32[64,1,128]{2,1,0:T(1,128)} %reshape.66), calls=%async_computation.5 | async-start | bytes 65536 | tf_op jit(solution)/shard_map/all_to_all | solution.py:39
  314.1 12.6 %all-to-all-done.5 = f32[64,1,128]{2,1,0:T(1,128)S(1)} async-done(((f32[64,1,128]{2,1,0:T(1,128)}), f32[64,1,128]{2,1,0:T(1,128)S(1)}, u32[]{:S(2)}, u32[]{:S(2)}) %all-to-all-start.5) | async-done | bytes 32800 | tf_op jit(solution)/shard_map/all_to_all | solution.py:39
  (95 shorter events, 87.4 us)
Async XLA Ops:
  0.6 10.3 %copy-start = (bf16[1,1024,100]{1,2,0:T(8,128)(2,1)S(1)}, bf16[1,1024,100]{1,2,0:T(8,128)(2,1)}, u32[]{:S(2)}) copy-start(bf16[1,1024,100]{1,2,0:T(8,128)(2,1)} %param.55) | copy-start | bytes 614404
  2.1 12.9 %all-to-all-start.1 = ((bf16[8,32,256]{2,1,0:T(8,128)(2,1)}), bf16[8,32,256]{2,1,0:T(8,128)(2,1)S(1)}, u32[]{:S(2)}, u32[]{:S(2)}) async-start(bf16[8,32,256]{2,1,0:T(8,128)(2,1)} %broadcast_in_dim.40), calls=%async_computation.1 | async-start | bytes 262144 | tf_op jit(solution)/shard_map/all_to_all | solution.py:18
  15.8 58.2 %all-to-all-start = ((bf16[8,1024,32]{1,2,0:T(8,128)(2,1)}), bf16[8,1024,32]{1,2,0:T(8,128)(2,1)S(1)}, u32[]{:S(2)}, u32[]{:S(2)}) async-start(bf16[8,1024,32]{1,2,0:T(8,128)(2,1)} %broadcast_in_dim.39), calls=%async_computation | async-start | bytes 1048576 | tf_op jit(solution)/shard_map/all_to_all | solution.py:18
  74.1 87.0 %all-to-all-start.3 = ((f32[8,1024,32]{1,2,0:T(8,128)}), f32[8,1024,32]{1,2,0:T(8,128)S(1)}, u32[]{:S(2)}, u32[]{:S(2)}) async-start(f32[8,1024,32]{1,2,0:T(8,128)} %bitcast.236), calls=%async_computation.3 | async-start | bytes 2097152 | tf_op jit(solution)/shard_map/all_to_all | solution.py:39
  161.9 59.3 %all-to-all-start.2 = ((bf16[8,1024,32]{1,2,0:T(8,128)(2,1)}), bf16[8,1024,32]{1,2,0:T(8,128)(2,1)S(1)}, u32[]{:S(2)}, u32[]{:S(2)}) async-start(bf16[8,1024,32]{1,2,0:T(8,128)(2,1)} %broadcast_in_dim.41), calls=%async_computation.2 | async-start | bytes 1048576 | tf_op jit(solution)/shard_map/all_to_all | solution.py:18
  222.1 44.7 %all-to-all-start.4 = ((bf16[8,1024,32]{1,2,0:T(8,128)(2,1)}), bf16[8,1024,32]{1,2,0:T(8,128)(2,1)S(1)}, u32[]{:S(2)}, u32[]{:S(2)}) async-start(bf16[8,1024,32]{1,2,0:T(8,128)(2,1)} %broadcast_in_dim.43), calls=%async_computation.4 | async-start | bytes 1048576 | tf_op jit(solution)/shard_map/all_to_all | solution.py:18
  268.3 58.4 %all-to-all-start.5 = ((f32[64,1,128]{2,1,0:T(1,128)}), f32[64,1,128]{2,1,0:T(1,128)S(1)}, u32[]{:S(2)}, u32[]{:S(2)}) async-start(f32[64,1,128]{2,1,0:T(1,128)} %reshape.66), calls=%async_computation.5 | async-start | bytes 65536 | tf_op jit(solution)/shard_map/all_to_all | solution.py:39
where the time goes:
time: 330 us; the launch traced here: 329 us
  starting transfers between devices  126 us (38%)
  local copies, waits for them, and re-layouts  57.4 us (17%)
  loops' own time  52.1 us (16%)
  waiting for transfers between devices  42.3 us (13%)
  matrix products  21 us (6%)
  blocking collectives  14.7 us (4%)
  between operations  11.4 us (3%)
  other arithmetic  3.94 us (1%)
    all_to_all x2, starting transfers between devices, summed_on_arrival(): lax.all_to_all(tiles, axis, split_axis=0, concat_axis=0, tiled=True)  70.8 us
    all_to_all x4, starting transfers between devices, sent_to_all(): return lax.all_to_all(copies, axis, split_axis=0, concat_axis=0, tiled=True)  55.1 us
    another operation x16, loops' own time, fold_slabs(): acc = lax.cond(valid, fold_apply, lambda total: total, acc)  35.1 us
    all_to_all x4, waiting for transfers between devices, sent_to_all(): return lax.all_to_all(copies, axis, split_axis=0, concat_axis=0, tiled=True)  29.6 us
    another operation x8, loops' own time, body(): term_rows = lax.cond(valid, spread_apply, lambda total: total, term_rows)  17 us
    dynamic_update_slice x10, local copies, waits for them, and re-layouts, fold_apply(): lax.dynamic_update_slice_in_dim(total, current + term, target[slot], 0)  15.4 us
    all_gather x2, blocking collectives, whole_of(): x = lax.all_gather(x, axis, axis=dim, tiled=True)  14.7 us
    another operation x10, local copies, waits for them, and re-layouts  13.9 us
  transfers between devices with their start and end apart: 6, of which 3 were waited for; matrix products, arithmetic and copies ran while one was open for 23% of the time, Pallas kernels for 0%

commit v1 on v0

v1 whole, which is shorter than its diff:
```python
import functools

import jax
import jax.numpy as jnp
from jax import lax
from jax.experimental import pallas as pl
from jax.experimental.pallas import tpu as pltpu
from jax.sharding import PartitionSpec as P

F32 = jnp.float32
BF16 = jnp.bfloat16
MESH = pl.DeviceIdType.MESH
NT = (((1,), (1,)), ((), ()))
CHUNKS = 4


def gelu(v):
    return 0.5 * v * (1.0 + jnp.tanh(0.7978845608028654 * (v + 0.044715 * (v * v * v))))


def kernel(
    dims,
    list_ref, count_ref, feat_hbm, win_hbm, wh_hbm, blocks_hbm, ct_hbm,
    out_ref, grad_ref,
    feat, win, blocks, z1, z2, ctb, ctp, wb, wct, gb, pb, rb, zb, zr,
    local_sem, line_send, line_recv, in_send, in_recv, ring_send, ring_recv,
    x_send, x_recv, z_send, z_recv,
):
    n_dom, n_col, n_x = dims
    n_y, n_z = n_col // 2, 2 * n_dom
    dom, col, rep = lax.axis_index("dom"), lax.axis_index("col"), lax.axis_index("rep")
    y, core = col // 2, col % 2
    z_hi, x = rep // n_x, rep % n_x
    z = z_hi * n_dom + dom

    def on_z(step):
        there = lax.rem(z + step, n_z)
        return {"dom": lax.rem(there, n_dom), "rep": (there // n_dom) * n_x + x}

    def on_x(step):
        return {"rep": z_hi * n_x + lax.rem(x + step, n_x)}

    def on_col(step):
        return {"col": lax.rem(col + step, n_col)}

    def on_y(step):
        return {"col": 2 * lax.rem(y + step, n_y) + core}

    sibling = {"col": 2 * y + 1 - core}

    def send(src, dst, send_sem, recv_sem, device):
        return pltpu.make_async_remote_copy(
            src_ref=src, dst_ref=dst, send_sem=send_sem, recv_sem=recv_sem,
            device_id=device, device_id_type=MESH,
        )

    barrier = pltpu.get_barrier_semaphore()
    for steps, place in ((n_z, on_z), (n_x, on_x), (n_col, on_col)):
        def greet(step, carry, place=place):
            pl.semaphore_signal(barrier, inc=1, device_id=place(step), device_id_type=MESH)
            return carry

        lax.fori_loop(1, steps, greet, 0)

    loads = [
        pltpu.make_async_copy(feat_hbm, feat, local_sem.at[0]),
        pltpu.make_async_copy(win_hbm, win, local_sem.at[1]),
        pltpu.make_async_copy(ct_hbm, ctb.at[col], local_sem.at[2]),
        pltpu.make_async_copy(wh_hbm, wb.at[col], local_sem.at[3]),
        pltpu.make_async_copy(blocks_hbm, blocks, local_sem.at[4]),
    ]
    for load in loads:
        load.start()

    def line_copy(e, buf, src, chunk, way):
        part = buf.at[2 * src + chunk // 2, chunk % 2]
        there = dom + 1 if way == 0 else dom - 1
        return send(
            part, part, line_send.at[e, way, src, chunk], line_recv.at[e, src, chunk],
            {"dom": there},
        )

    def line_start(e, buf):
        for chunk in range(CHUNKS):
            @pl.when(dom < n_dom - 1)
            def _():
                line_copy(e, buf, dom, chunk, 0).start()

            @pl.when(dom > 0)
            def _():
                line_copy(e, buf, dom, chunk, 1).start()

    def line_pass(e, buf):
        def step(s, carry):
            for chunk in range(CHUNKS):
                @pl.when(dom - s >= 0)
                def _():
                    line_copy(e, buf, dom - s, chunk, 0).wait_recv()

                    @pl.when(dom < n_dom - 1)
                    def _():
                        line_copy(e, buf, dom - s, chunk, 0).start()

                @pl.when(dom + s < n_dom)
                def _():
                    line_copy(e, buf, dom + s, chunk, 1).wait_recv()

                    @pl.when(dom > 0)
                    def _():
                        line_copy(e, buf, dom + s, chunk, 1).start()
            return carry

        lax.fori_loop(1, n_dom, step, 0)

    def line_drain(e, buf):
        def step(src, carry):
            for chunk in range(CHUNKS):
                @pl.when((src <= dom) & (dom < n_dom - 1))
                def _():
                    line_copy(e, buf, src, chunk, 0).wait_send()

                @pl.when((src >= dom) & (dom > 0))
                def _():
                    line_copy(e, buf, src, chunk, 1).wait_send()
            return carry

        lax.fori_loop(0, n_dom, step, 0)

    def gather_copy(a, buf, step):
        return send(buf.at[col], buf.at[col], in_send.at[a, step], in_recv.at[a, col], on_col(step))

    def gather_arrival(a, buf, step):
        src = lax.rem(col + step, n_col)
        return send(buf.at[src], buf.at[src], in_send.at[a, step], in_recv.at[a, src], on_col(step))

    def spread(buf):
        total = jnp.zeros((64, 512), F32)
        for slot in range(8):
            used = slot < count_ref[0, 0]
            row = list_ref[0, slot]
            part = buf[2 * list_ref[1, slot] + list_ref[2, slot]].reshape(32, 512).astype(F32)
            first = jnp.where(used & (row == 0), 1.0, 0.0)
            second = jnp.where(used & (row == 1), 1.0, 0.0)
            both = jnp.concatenate([part * first, part * second], axis=0).astype(BF16)
            total = total + lax.dot_general(both, blocks[slot], NT, preferred_element_type=F32)
        return total

    loads[0].wait()
    loads[1].wait()
    own = jnp.dot(win[...], feat[...], preferred_element_type=F32).astype(BF16)
    for j in range(2):
        for h in range(2):
            z1[2 * dom + j, h] = own[16 * h : 16 * h + 16, 512 * j : 512 * j + 512]

    pl.semaphore_wait(barrier, (n_z - 1) + (n_x - 1) + (n_col - 1))
    line_start(0, z1)

    loads[2].wait()
    loads[3].wait()
    for a, buf in ((0, wb), (1, ctb)):
        def start(step, carry, a=a, buf=buf):
            gather_copy(a, buf, step).start()
            return carry

        lax.fori_loop(1, n_col, start, 0)

    line_pass(0, z1)
    loads[4].wait()
    h1 = gelu(spread(z1)).astype(BF16)
    for j in range(2):
        for h in range(2):
            z2[2 * dom + j, h] = h1[32 * j + 16 * h : 32 * j + 16 * h + 16]
    line_start(1, z2)

    for a, buf in ((0, wb), (1, ctb)):
        def arrive(step, carry, a=a, buf=buf):
            gather_arrival(a, buf, step).wait_recv()
            return carry

        lax.fori_loop(1, n_col, arrive, 0)
    units = lax.broadcasted_iota(jnp.int32, (32, 256), 0) + 32 * col
    pick = (lax.broadcasted_iota(jnp.int32, (32, 256), 1) == units).astype(F32).astype(BF16)
    wct[...] = lax.dot_general(
        pick, wb[...].reshape(256, 256), NT, preferred_element_type=F32
    ).astype(BF16)
    place = lax.broadcasted_iota(jnp.int32, (256, 256), 0)
    wanted = 32 * (place & 7) + 16 * ((place >> 3) & 1) + 4 * ((place >> 4) & 3) + (place >> 6)
    order = (lax.broadcasted_iota(jnp.int32, (256, 256), 1) == wanted).astype(F32).astype(BF16)
    ctp[...] = jnp.dot(
        order, ctb[...].reshape(256, 1024), preferred_element_type=F32
    ).astype(BF16)

    line_pass(1, z2)
    g = spread(z2).astype(BF16)
    for j in range(2):
        for h in range(2):
            gb[col, h, :, 512 * j : 512 * j + 512] = g[32 * j + 16 * h : 32 * j + 16 * h + 16]

    def ring_copy(index, src, h, device):
        part = gb.at[src] if h is None else gb.at[src, h]
        return send(part, part, ring_send.at[index], ring_recv.at[index], device)

    before = 2 * lax.rem(y + n_y - 1, n_y) + core
    after = 2 * lax.rem(y + 1, n_y) + core
    across = 2 * lax.rem(y + 2, n_y) + core
    up, down = on_y(1), on_y(n_y - 1)
    other = 1 - 2 * core
    first = [
        ring_copy(0, col, 0, up), ring_copy(1, col, 1, down),
        ring_copy(2, col, 1, up), ring_copy(3, col, 0, down),
        ring_copy(4, col, None, sibling),
    ]
    for copy in first:
        copy.start()

    ga = gb[col].reshape(32, 1024)
    part = lax.dot_general(ctp[...], ga, NT, preferred_element_type=F32)
    packed = jnp.concatenate([part[64 * q : 64 * q + 64] for q in range(4)], axis=1)
    for t in range(n_x):
        pb[t] = packed[16 * t : 16 * t + 16]

    def x_copy(step):
        return send(
            pb.at[lax.rem(x + step, n_x)], rb.at[step], x_send.at[step], x_recv.at[step], on_x(step)
        )

    for step in range(1, n_x):
        x_copy(step).start()

    ring_copy(0, before, 0, up).wait_recv()
    second = [ring_copy(5, before, 0, up)]
    second[0].start()
    ring_copy(1, after, 1, down).wait_recv()
    second.append(ring_copy(6, after, 1, down))
    second[1].start()
    ring_copy(2, before, 1, up).wait_recv()
    second.append(ring_copy(7, before, None, sibling))
    second[2].start()
    ring_copy(3, after, 0, down).wait_recv()
    second.append(ring_copy(8, after, None, sibling))
    second[3].start()

    sums = pb[x]
    for step in range(1, n_x):
        x_copy(step).wait_recv()
        sums = sums + rb[step]
    for t in range(n_z):
        zb[t] = sums[t : t + 1]

    def z_copy(step):
        return send(
            zb.at[lax.rem(z + step, n_z)], zr.at[step], z_send.at[step], z_recv.at[step], on_z(step)
        )

    def z_start(step, carry):
        z_copy(step).start()
        return carry

    lax.fori_loop(1, n_z, z_start, 0)

    ring_copy(5, across, 0, up).wait_recv()
    third = [ring_copy(9, across, 0, sibling)]
    third[0].start()
    ring_copy(6, across, 1, down).wait_recv()
    third.append(ring_copy(10, across, 1, sibling))
    third[1].start()
    ring_copy(4, col + other, None, sibling).wait_recv()
    ring_copy(7, before + other, None, sibling).wait_recv()
    ring_copy(8, after + other, None, sibling).wait_recv()
    ring_copy(9, across + other, 0, sibling).wait_recv()
    ring_copy(10, across + other, 1, sibling).wait_recv()
    out_ref[...] = jnp.dot(
        wct[...], gb[...].reshape(256, 1024), preferred_element_type=F32
    ).astype(BF16)

    def z_add(step, total):
        z_copy(step).wait_recv()
        return total + zr[step]

    total = lax.fori_loop(1, n_z, z_add, zb[z])
    for q in range(4):
        grad_ref[q : q + 1, :] = total[:, 32 * q : 32 * q + 32]

    for copy in first + second + third:
        copy.wait_send()
    for step in range(1, n_x):
        x_copy(step).wait_send()

    def z_done(step, carry):
        z_copy(step).wait_send()
        return carry

    lax.fori_loop(1, n_z, z_done, 0)
    for a, buf in ((0, wb), (1, ctb)):
        def done(step, carry, a=a, buf=buf):
            gather_copy(a, buf, step).wait_send()
            return carry

        lax.fori_loop(1, n_col, done, 0)
    line_drain(0, z1)
    line_drain(1, z2)


def solution(mesh):
    n_dom, n_col = mesh.shape["dom"], mesh.shape["col"]
    n_x = mesh.shape["rep"] // 2
    dims = (n_dom, n_col, n_x)
    n_z = 2 * n_dom

    def body(features, w_in, w_hidden, blocks, block_list, block_count, cotangent):
        hbm = pl.BlockSpec(memory_space=pltpu.HBM)
        smem = pl.BlockSpec(memory_space=pltpu.SMEM)
        vmem = pl.BlockSpec(memory_space=pltpu.VMEM)
        dma = pltpu.SemaphoreType.DMA
        out, grad = pl.pallas_call(
            functools.partial(kernel, dims),
            out_shape=(
                jax.ShapeDtypeStruct((32, 1024), BF16),
                jax.ShapeDtypeStruct((4, 32), F32),
            ),
            in_specs=[smem, smem, hbm, hbm, hbm, hbm, hbm],
            out_specs=(vmem, vmem),
            scratch_shapes=[
                pltpu.VMEM((100, 1024), BF16),
                pltpu.VMEM((32, 100), BF16),
                pltpu.VMEM((8, 512, 512), BF16),
                pltpu.VMEM((2 * n_dom, 2, 16, 512), BF16),
                pltpu.VMEM((2 * n_dom, 2, 16, 512), BF16),
                pltpu.VMEM((n_col, 32, 1024), BF16),
                pltpu.VMEM((256, 1024), BF16),
                pltpu.VMEM((n_col, 32, 256), BF16),
                pltpu.VMEM((32, 256), BF16),
                pltpu.VMEM((n_col, 2, 16, 1024), BF16),
                pltpu.VMEM((n_x, 16, 128), F32),
                pltpu.VMEM((n_x, 16, 128), F32),
                pltpu.VMEM((n_z, 1, 128), F32),
                pltpu.VMEM((n_z, 1, 128), F32),
                dma((5,)),
                dma((2, 2, n_dom, CHUNKS)),
                dma((2, n_dom, CHUNKS)),
                dma((2, n_col)),
                dma((2, n_col)),
                dma((11,)),
                dma((11,)),
                dma((n_x,)),
                dma((n_x,)),
                dma((n_z,)),
                dma((n_z,)),
            ],
            compiler_params=pltpu.CompilerParams(collective_id=0, has_side_effects=True),
        )(
            block_list[0, 0].T,
            block_count,
            features[0].T,
            w_in.T,
            w_hidden,
            blocks[0, 0],
            cotangent[0].T,
        )
        return out.T[None], grad.T

    return jax.shard_map(
        body,
        mesh=mesh,
        in_specs=(
            P("rep", "dom", None),
            P(None, "col"),
            P("col", None),
            P("rep", "dom", None, None, None),
            P("rep", "dom", None, None),
            P("rep", "dom"),
            P("rep", "dom", "col"),
        ),
        out_specs=(P("rep", "dom", "col"), P("col", ("dom", "rep"))),
        check_vma=False,
    )
```

time: 330 us -> 81.4 us (0.25)
  starting transfers between devices: 126 us -> 0 us
  Pallas kernels: 0 us -> 75.7 us
  local copies, waits for them, and re-layouts: 57.4 us -> 3.98 us
  loops' own time: 52.1 us -> 0 us
  waiting for transfers between devices: 42.3 us -> 0 us
  matrix products: 21 us -> 0 us
  blocking collectives: 14.7 us -> 0 us
  between operations: 11.4 us -> 1.29 us
  other arithmetic: 3.94 us -> 0 us
    all_to_all x6 -> x0, starting transfers between devices: 126 us -> none  [the longest x2 70.8 us: summed_on_arrival(): lax.all_to_all(tiles, axis, split_axis=0, concat_axis=0, tiled=True)]
    pallas_call x0 -> x1, Pallas kernels: none -> 75.7 us  [body(): pl.pallas_call(functools.partial(kernel, dims), out_shape=(jax.ShapeDtype...]
    another operation x24 -> x0, loops' own time: 52.1 us -> none  [the longest x16 35.1 us: fold_slabs(): acc = lax.cond(valid, fold_apply, lambda total: total, acc)]
    all_to_all x6 -> x0, waiting for transfers between devices: 42.3 us -> none  [the longest x4 29.6 us: sent_to_all(): return lax.all_to_all(copies, axis, split_axis=0, concat_axis=0, tiled=True)]
    dynamic_update_slice x15 -> x0, local copies, waits for them, and re-layouts: 23.3 us -> none  [the longest x10 15.4 us: fold_apply(): lax.dynamic_update_slice_in_dim(total, current + term, target[slot], 0)]
    dot_general x18 -> x0, matrix products: 21 us -> none  [the longest x10 13.3 us: fold_apply(): term = jnp.dot(local_blocks[slot], part, preferred_element_type=jnp.float32)]
    all_gather x2 -> x0, blocking collectives: 14.7 us -> none  [whole_of(): x = lax.all_gather(x, axis, axis=dim, tiled=True)]
    another operation x10 -> x0, local copies, waits for them, and re-layouts: 13.9 us -> none
  transfers between devices with their start and end apart: 6 -> 0, of which waited for: 3 -> 0; matrix products, arithmetic and copies ran while one was open for 23% -> 0% of each run, Pallas kernels for 0% -> 0%
where the time goes in v1:
time: 81.4 us; the launch traced here: 80.9 us
  Pallas kernels  75.7 us (93%)
  local copies, waits for them, and re-layouts  3.98 us (5%)
  between operations  1.29 us (2%)
    pallas_call x1, Pallas kernels, body(): pl.pallas_call(functools.partial(kernel, dims), out_shape=(jax.ShapeDtype...  75.7 us
    unnamed x3, local copies, waits for them, and re-layouts  3.98 us

profile of v1, /device:TPU:24, one launch (start us, length us, event | category | flops | bytes accessed | tf_op | source)
XLA Modules:
  0.0 80.9 jit_solution(13756080561403310443)
XLA Ops:
  1.3 1.3 %copy.11 = s32[1,1,8,3]{2,3,1,0:T(4,128)} copy(s32[1,1,8,3]{2,1,3,0:T(1,128)} %param.11) | data formatting | bytes 192
  2.5 75.7 %shard_map.86 = (bf16[32,1024]{1,0:T(8,128)(2,1)}, f32[4,32]{1,0:T(4,128)}) custom-call(s32[3,8]{1,0:T(4,128)} %bitcast.22, s32[1,1]{1,0:T(1,128)S(6)} %copy.14.count_ref, bf16[100,1024]{1,0:T(8,128)(2,1)} %bitcast.18, bf16[32,100]{1,0:T(8,128)(2,1)} %bitcast.21, bf16[32,256]{1,0:T(8,128)(2,1)} %wh_hbm.1, bf16[8,512,512]{2,1,0:T(8,128)(2,1)} %bitcast.17, ...), custom_call_target="tpu_custom_call" | custom-call | tf_op jit(solution)/shard_map/pallas_call | solution.py:315
  78.2 1.5 %copy.15 = bf16[1,1024,32]{1,2,0:T(8,128)(2,1)} copy(bf16[1,1024,32]{1,2,0:T(8,128)(2,1)} %bitcast.20) | data formatting | bytes 131072
  79.7 1.2 %copy.16 = f32[32,4]{0,1:T(4,128)} copy(f32[32,4]{0,1:T(4,128)} %bitcast.23) | data formatting | bytes 1024

commit v2 on v1

--- a/solution.py
+++ b/solution.py
@@ -11,7 +11,18 @@
 BF16 = jnp.bfloat16
 MESH = pl.DeviceIdType.MESH
 NT = (((1,), (1,)), ((), ()))
-CHUNKS = 4
+CHUNKS = 2
+PROGRAMS = {
+    0: (('s', 0, 0, 2), ('s', 0, 0, 1), ('s', 0, 1, 2), ('s', 0, 1, 1), ('w', 1, 0, -1), ('w', 1, 1, -1), ('w', 2, 0, -1), ('w', 2, 1, -1), ('w', 3, 0, -1), ('w', 4, 0, -1), ('w', 3, 1, -1), ('w', 4, 1, -1), ('w', 5, 0, -1), ('w', 6, 0, -1), ('w', 5, 1, -1), ('w', 6, 1, -1), ('w', 7, 0, -1), ('w', 7, 1, -1)),
+    1: (('s', 1, 0, 3), ('s', 1, 0, 2), ('s', 1, 0, 0), ('s', 1, 1, 3), ('s', 1, 1, 2), ('s', 1, 1, 0), ('w', 0, 0, -1), ('w', 2, 0, -1), ('w', 0, 1, -1), ('w', 2, 1, -1), ('w', 3, 0, -1), ('s', 3, 0, 0), ('w', 3, 1, -1), ('s', 3, 1, 0), ('w', 4, 0, -1), ('w', 5, 0, -1), ('s', 5, 0, 0), ('w', 4, 1, -1), ('w', 5, 1, -1), ('s', 5, 1, 0), ('w', 6, 0, -1), ('w', 7, 0, -1), ('s', 7, 0, 0), ('w', 6, 1, -1), ('w', 7, 1, -1), ('s', 7, 1, 0)),
+    2: (('s', 2, 0, 4), ('s', 2, 0, 0), ('s', 2, 0, 3), ('s', 2, 0, 1), ('s', 2, 1, 4), ('s', 2, 1, 0), ('s', 2, 1, 3), ('s', 2, 1, 1), ('w', 0, 0, -1), ('s', 0, 0, 4), ('s', 0, 0, 3), ('w', 3, 0, -1), ('w', 0, 1, -1), ('s', 0, 1, 4), ('s', 0, 1, 3), ('w', 3, 1, -1), ('w', 1, 0, -1), ('w', 4, 0, -1), ('s', 4, 0, 0), ('s', 4, 0, 1), ('w', 4, 1, -1), ('s', 4, 1, 0), ('s', 4, 1, 1), ('w', 1, 1, -1), ('w', 5, 0, -1), ('w', 6, 0, -1), ('s', 6, 0, 0), ('s', 6, 0, 1), ('w', 5, 1, -1), ('w', 6, 1, -1), ('s', 6, 1, 0), ('s', 6, 1, 1), ('w', 7, 0, -1), ('w', 7, 1, -1)),
+    3: (('s', 3, 0, 5), ('s', 3, 0, 1), ('s', 3, 0, 4), ('s', 3, 0, 2), ('s', 3, 1, 5), ('s', 3, 1, 1), ('s', 3, 1, 4), ('s', 3, 1, 2), ('w', 4, 0, -1), ('w', 4, 1, -1), ('w', 1, 0, -1), ('s', 1, 0, 5), ('s', 1, 0, 4), ('w', 5, 0, -1), ('s', 5, 0, 1), ('s', 5, 0, 2), ('w', 1, 1, -1), ('s', 1, 1, 5), ('s', 1, 1, 4), ('w', 5, 1, -1), ('s', 5, 1, 1), ('s', 5, 1, 2), ('w', 2, 0, -1), ('w', 2, 1, -1), ('w', 6, 0, -1), ('w', 0, 0, -1), ('w', 7, 0, -1), ('s', 7, 0, 1), ('s', 7, 0, 2), ('w', 6, 1, -1), ('w', 0, 1, -1), ('w', 7, 1, -1), ('s', 7, 1, 1), ('s', 7, 1, 2)),
+    4: (('s', 4, 0, 6), ('s', 4, 0, 2), ('s', 4, 0, 5), ('s', 4, 0, 3), ('s', 4, 1, 6), ('s', 4, 1, 2), ('s', 4, 1, 5), ('s', 4, 1, 3), ('w', 5, 0, -1), ('w', 5, 1, -1), ('w', 6, 0, -1), ('s', 6, 0, 2), ('s', 6, 0, 3), ('w', 6, 1, -1), ('s', 6, 1, 2), ('s', 6, 1, 3), ('w', 2, 0, -1), ('s', 2, 0, 6), ('s', 2, 0, 5), ('w', 2, 1, -1), ('s', 2, 1, 6), ('s', 2, 1, 5), ('w', 7, 0, -1), ('w', 3, 0, -1), ('w', 7, 1, -1), ('w', 3, 1, -1), ('w', 0, 0, -1), ('s', 0, 0, 6), ('s', 0, 0, 5), ('w', 0, 1, -1), ('s', 0, 1, 6), ('s', 0, 1, 5), ('w', 1, 0, -1), ('w', 1, 1, -1)),
+    5: (('s', 5, 0, 3), ('s', 5, 0, 7), ('s', 5, 0, 6), ('s', 5, 0, 4), ('s', 5, 1, 3), ('s', 5, 1, 7), ('s', 5, 1, 6), ('s', 5, 1, 4), ('w', 6, 0, -1), ('w', 6, 1, -1), ('w', 7, 0, -1), ('s', 7, 0, 3), ('s', 7, 0, 4), ('w', 7, 1, -1), ('s', 7, 1, 3), ('s', 7, 1, 4), ('w', 3, 0, -1), ('s', 3, 0, 7), ('s', 3, 0, 6), ('w', 3, 1, -1), ('s', 3, 1, 7), ('s', 3, 1, 6), ('w', 4, 0, -1), ('w', 4, 1, -1), ('w', 1, 0, -1), ('s', 1, 0, 7), ('s', 1, 0, 6), ('w', 1, 1, -1), ('s', 1, 1, 7), ('s', 1, 1, 6), ('w', 2, 0, -1), ('w', 2, 1, -1), ('w', 0, 0, -1), ('w', 0, 1, -1)),
+    6: (('s', 6, 0, 4), ('s', 6, 0, 7), ('s', 6, 0, 5), ('s', 6, 1, 4), ('s', 6, 1, 7), ('s', 6, 1, 5), ('w', 7, 0, -1), ('w', 7, 1, -1), ('w', 4, 0, -1), ('s', 4, 0, 7), ('w', 4, 1, -1), ('s', 4, 1, 7), ('w', 5, 0, -1), ('w', 5, 1, -1), ('w', 2, 0, -1), ('s', 2, 0, 7), ('w', 2, 1, -1), ('s', 2, 1, 7), ('w', 3, 0, -1), ('w', 3, 1, -1), ('w', 0, 0, -1), ('s', 0, 0, 7), ('w', 0, 1, -1), ('s', 0, 1, 7), ('w', 1, 0, -1), ('w', 1, 1, -1)),
+    7: (('s', 7, 0, 5), ('s', 7, 0, 6), ('s', 7, 1, 5), ('s', 7, 1, 6), ('w', 5, 0, -1), ('w', 5, 1, -1), ('w', 6, 0, -1), ('w', 6, 1, -1), ('w', 3, 0, -1), ('w', 3, 1, -1), ('w', 4, 0, -1), ('w', 4, 1, -1), ('w', 1, 0, -1), ('w', 1, 1, -1), ('w', 2, 0, -1), ('w', 2, 1, -1), ('w', 0, 0, -1), ('w', 0, 1, -1)),
+}
+PARTNERS = {0: (1, 2), 1: (0, 2, 3), 2: (0, 1, 3, 4), 3: (1, 2, 4, 5), 4: (2, 3, 5, 6), 5: (3, 4, 6, 7), 6: (4, 5, 7), 7: (5, 6)}
 
 
 def gelu(v):
@@ -20,11 +31,11 @@
 
 def kernel(
     dims,
-    list_ref, count_ref, feat_hbm, win_hbm, wh_hbm, blocks_hbm, ct_hbm,
+    list_hbm, count_hbm, feat_hbm, win_hbm, wh_hbm, blocks_hbm, ct_hbm,
     out_ref, grad_ref,
     feat, win, blocks, z1, z2, ctb, ctp, wb, wct, gb, pb, rb, zb, zr,
     local_sem, line_send, line_recv, in_send, in_recv, ring_send, ring_recv,
-    x_send, x_recv, z_send, z_recv,
+    x_send, x_recv, z_send, z_recv, entered, lists, count,
 ):
     n_dom, n_col, n_x = dims
     n_y, n_z = n_col // 2, 2 * n_dom
@@ -55,12 +66,23 @@
         )
 
     barrier = pltpu.get_barrier_semaphore()
-    for steps, place in ((n_z, on_z), (n_x, on_x), (n_col, on_col)):
+    for steps, place in ((n_x, on_x), (n_col, on_col)):
         def greet(step, carry, place=place):
             pl.semaphore_signal(barrier, inc=1, device_id=place(step), device_id_type=MESH)
             return carry
 
         lax.fori_loop(1, steps, greet, 0)
+    for v in range(n_dom):
+        @pl.when(dom == v)
+        def _(v=v):
+            for partner in PARTNERS[v]:
+                pl.semaphore_signal(
+                    barrier, inc=1, device_id={"dom": partner}, device_id_type=MESH
+                )
+            if v == 0:
+                pl.semaphore_signal(barrier, inc=1, device_id=on_z(n_z - 1), device_id_type=MESH)
+            if v == n_dom - 1:
+                pl.semaphore_signal(barrier, inc=1, device_id=on_z(1), device_id_type=MESH)
 
     loads = [
         pltpu.make_async_copy(feat_hbm, feat, local_sem.at[0]),
@@ -68,63 +90,57 @@
         pltpu.make_async_copy(ct_hbm, ctb.at[col], local_sem.at[2]),
         pltpu.make_async_copy(wh_hbm, wb.at[col], local_sem.at[3]),
         pltpu.make_async_copy(blocks_hbm, blocks, local_sem.at[4]),
+        pltpu.make_async_copy(list_hbm, lists, local_sem.at[5]),
+        pltpu.make_async_copy(count_hbm, count, local_sem.at[6]),
     ]
     for load in loads:
         load.start()
 
-    def line_copy(e, buf, src, chunk, way):
-        part = buf.at[2 * src + chunk // 2, chunk % 2]
-        there = dom + 1 if way == 0 else dom - 1
+    def piece(buf, src, chunk):
+        if CHUNKS == 1:
+            return buf.at[2 * src : 2 * src + 2]
+        return buf.at[2 * src + chunk]
+
+    def line_copy(e, buf, src, chunk, dst):
+        part = piece(buf, src, chunk)
         return send(
-            part, part, line_send.at[e, way, src, chunk], line_recv.at[e, src, chunk],
-            {"dom": there},
+            part, part, line_send.at[e, src, chunk, dst], line_recv.at[e, src, chunk], {"dom": dst}
         )
 
+    def for_each_place(steps):
+        for v in range(n_dom):
+            @pl.when(dom == v)
+            def _(v=v):
+                steps(v, PROGRAMS[v])
+
     def line_start(e, buf):
-        for chunk in range(CHUNKS):
-            @pl.when(dom < n_dom - 1)
-            def _():
-                line_copy(e, buf, dom, chunk, 0).start()
-
-            @pl.when(dom > 0)
-            def _():
-                line_copy(e, buf, dom, chunk, 1).start()
+        def steps(v, program):
+            for kind, src, chunk, dst in program:
+                if kind == "w":
+                    return
+                line_copy(e, buf, src, chunk, dst).start()
+
+        for_each_place(steps)
 
     def line_pass(e, buf):
-        def step(s, carry):
-            for chunk in range(CHUNKS):
-                @pl.when(dom - s >= 0)
-                def _():
-                    line_copy(e, buf, dom - s, chunk, 0).wait_recv()
-
-                    @pl.when(dom < n_dom - 1)
-                    def _():
-                        line_copy(e, buf, dom - s, chunk, 0).start()
-
-                @pl.when(dom + s < n_dom)
-                def _():
-                    line_copy(e, buf, dom + s, chunk, 1).wait_recv()
-
-                    @pl.when(dom > 0)
-                    def _():
-                        line_copy(e, buf, dom + s, chunk, 1).start()
-            return carry
-
-        lax.fori_loop(1, n_dom, step, 0)
+        def steps(v, program):
+            waited = False
+            for kind, src, chunk, dst in program:
+                waited = waited or kind == "w"
+                if kind == "w":
+                    line_copy(e, buf, src, chunk, v).wait_recv()
+                elif waited:
+                    line_copy(e, buf, src, chunk, dst).start()
+
+        for_each_place(steps)
 
     def line_drain(e, buf):
-        def step(src, carry):
-            for chunk in range(CHUNKS):
-                @pl.when((src <= dom) & (dom < n_dom - 1))
-                def _():
-                    line_copy(e, buf, src, chunk, 0).wait_send()
-
-                @pl.when((src >= dom) & (dom > 0))
-                def _():
-                    line_copy(e, buf, src, chunk, 1).wait_send()
-            return carry
-
-        lax.fori_loop(0, n_dom, step, 0)
+        def steps(v, program):
+            for kind, src, chunk, dst in program:
+                if kind == "s":
+                    line_copy(e, buf, src, chunk, dst).wait_send()
+
+        for_each_place(steps)
 
     def gather_copy(a, buf, step):
         return send(buf.at[col], buf.at[col], in_send.at[a, step], in_recv.at[a, col], on_col(step))
@@ -136,9 +152,9 @@
     def spread(buf):
         total = jnp.zeros((64, 512), F32)
         for slot in range(8):
-            used = slot < count_ref[0, 0]
-            row = list_ref[0, slot]
-            part = buf[2 * list_ref[1, slot] + list_ref[2, slot]].reshape(32, 512).astype(F32)
+            used = slot < count[0, 0]
+            row = lists[0, 0, 0, slot]
+            part = buf[2 * lists[0, 1, 0, slot] + lists[0, 2, 0, slot]].reshape(32, 512).astype(F32)
             first = jnp.where(used & (row == 0), 1.0, 0.0)
             second = jnp.where(used & (row == 1), 1.0, 0.0)
             both = jnp.concatenate([part * first, part * second], axis=0).astype(BF16)
@@ -152,7 +168,12 @@
         for h in range(2):
             z1[2 * dom + j, h] = own[16 * h : 16 * h + 16, 512 * j : 512 * j + 512]
 
-    pl.semaphore_wait(barrier, (n_z - 1) + (n_x - 1) + (n_col - 1))
+    for v in range(n_dom):
+        @pl.when(dom == v)
+        def _(v=v):
+            ends = 1 if v in (0, n_dom - 1) else 0
+            pl.semaphore_wait(barrier, len(PARTNERS[v]) + ends + (n_x - 1) + (n_col - 1))
+
     line_start(0, z1)
 
     loads[2].wait()
@@ -165,11 +186,22 @@
         lax.fori_loop(1, n_col, start, 0)
 
     line_pass(0, z1)
-    loads[4].wait()
+
+    @pl.when(dom == n_dom - 1)
+    def _():
+        pl.semaphore_signal(entered, inc=1, device_id=on_z(1), device_id_type=MESH)
+
+    for load in loads[4:]:
+        load.wait()
     h1 = gelu(spread(z1)).astype(BF16)
     for j in range(2):
         for h in range(2):
             z2[2 * dom + j, h] = h1[32 * j + 16 * h : 32 * j + 16 * h + 16]
+
+    @pl.when(dom == 0)
+    def _():
+        pl.semaphore_wait(entered, 1)
+
     line_start(1, z2)
 
     for a, buf in ((0, wb), (1, ctb)):
@@ -227,6 +259,24 @@
     for step in range(1, n_x):
         x_copy(step).start()
 
+    sums = pb[x]
+    for step in range(1, n_x):
+        x_copy(step).wait_recv()
+        sums = sums + rb[step]
+    for t in range(n_z):
+        zb[t] = sums[t : t + 1]
+
+    def z_copy(step):
+        return send(
+            zb.at[lax.rem(z + step, n_z)], zr.at[step], z_send.at[step], z_recv.at[step], on_z(step)
+        )
+
+    def z_start(step, carry):
+        z_copy(step).start()
+        return carry
+
+    lax.fori_loop(1, n_z, z_start, 0)
+
     ring_copy(0, before, 0, up).wait_recv()
     second = [ring_copy(5, before, 0, up)]
     second[0].start()
@@ -239,24 +289,6 @@
     ring_copy(3, after, 0, down).wait_recv()
     second.append(ring_copy(8, after, None, sibling))
     second[3].start()
-
-    sums = pb[x]
-    for step in range(1, n_x):
-        x_copy(step).wait_recv()
-        sums = sums + rb[step]
-    for t in range(n_z):
-        zb[t] = sums[t : t + 1]
-
-    def z_copy(step):
-        return send(
-            zb.at[lax.rem(z + step, n_z)], zr.at[step], z_send.at[step], z_recv.at[step], on_z(step)
-        )
-
-    def z_start(step, carry):
-        z_copy(step).start()
-        return carry
-
-    lax.fori_loop(1, n_z, z_start, 0)
 
     ring_copy(5, across, 0, up).wait_recv()
     third = [ring_copy(9, across, 0, sibling)]
@@ -309,7 +341,6 @@
 
     def body(features, w_in, w_hidden, blocks, block_list, block_count, cotangent):
         hbm = pl.BlockSpec(memory_space=pltpu.HBM)
-        smem = pl.BlockSpec(memory_space=pltpu.SMEM)
         vmem = pl.BlockSpec(memory_space=pltpu.VMEM)
         dma = pltpu.SemaphoreType.DMA
         out, grad = pl.pallas_call(
@@ -318,7 +349,7 @@
                 jax.ShapeDtypeStruct((32, 1024), BF16),
                 jax.ShapeDtypeStruct((4, 32), F32),
             ),
-            in_specs=[smem, smem, hbm, hbm, hbm, hbm, hbm],
+            in_specs=[hbm] * 7,
             out_specs=(vmem, vmem),
             scratch_shapes=[
                 pltpu.VMEM((100, 1024), BF16),
@@ -335,8 +366,8 @@
                 pltpu.VMEM((n_x, 16, 128), F32),
                 pltpu.VMEM((n_z, 1, 128), F32),
                 pltpu.VMEM((n_z, 1, 128), F32),
-                dma((5,)),
-                dma((2, 2, n_dom, CHUNKS)),
+                dma((7,)),
+                dma((2, n_dom, CHUNKS, n_dom)),
                 dma((2, n_dom, CHUNKS)),
                 dma((2, n_col)),
                 dma((2, n_col)),
@@ -346,10 +377,13 @@
                 dma((n_x,)),
                 dma((n_z,)),
                 dma((n_z,)),
+                pltpu.SemaphoreType.REGULAR,
+                pltpu.SMEM((1, 3, 1, 8), jnp.int32),
+                pltpu.SMEM((1, 1), jnp.int32),
             ],
             compiler_params=pltpu.CompilerParams(collective_id=0, has_side_effects=True),
         )(
-            block_list[0, 0].T,
+            jnp.transpose(block_list, (0, 3, 1, 2)),
             block_count,
             features[0].T,
             w_in.T,

time: 81.4 us -> 68.8 us (0.85)
  Pallas kernels: 75.7 us -> 63.8 us
  local copies, waits for them, and re-layouts: 3.98 us -> 2.72 us
    pallas_call x1, Pallas kernels: 75.7 us -> 63.8 us  [body(): pl.pallas_call(functools.partial(kernel, dims), out_shape=(jax.ShapeDtype...]
    unnamed x3 -> x2, local copies, waits for them, and re-layouts: 3.98 us -> 2.72 us
where the time goes in v2:
time: 68.8 us; the launch traced here: 67.8 us
  Pallas kernels  63.8 us (93%)
  local copies, waits for them, and re-layouts  2.72 us (4%)
  between operations  1.29 us (2%)
    pallas_call x1, Pallas kernels, body(): pl.pallas_call(functools.partial(kernel, dims), out_shape=(jax.ShapeDtype...  63.8 us
    unnamed x2, local copies, waits for them, and re-layouts  2.72 us

profile of v2, /device:TPU:24, one launch (start us, length us, event | category | flops | bytes accessed | tf_op | source)
XLA Modules:
  0.0 67.8 jit_solution(3730102800502692937)
XLA Ops:
  1.3 63.8 %shard_map.86 = (bf16[32,1024]{1,0:T(8,128)(2,1)}, f32[4,32]{1,0:T(4,128)}) custom-call(s32[1,3,1,8]{3,2,1,0:T(1,128)} %bitcast.19, s32[1,1]{1,0:T(1,128)S(6)} %copy.11.count_hbm, bf16[100,1024]{1,0:T(8,128)(2,1)} %bitcast.14, bf16[32,100]{1,0:T(8,128)(2,1)} %bitcast.17, bf16[32,256]{1,0:T(8,128)(2,1)} %wh_hbm.1, bf16[8,512,512]{2,1,0:T(8,128)(2,1)} %bitcast.13, ...), custom_call_target="tpu_custom_call" | custom-call | tf_op jit(solution)/shard_map/pallas_call | solution.py:346
  65.1 1.5 %copy.12 = bf16[1,1024,32]{1,2,0:T(8,128)(2,1)} copy(bf16[1,1024,32]{1,2,0:T(8,128)(2,1)} %bitcast.16) | data formatting | bytes 131072
  66.6 1.2 %copy.13 = f32[32,4]{0,1:T(4,128)} copy(f32[32,4]{0,1:T(4,128)} %bitcast.18) | data formatting | bytes 1024

commit v3 on v2

--- a/solution.py
+++ b/solution.py
@@ -11,18 +11,18 @@
 BF16 = jnp.bfloat16
 MESH = pl.DeviceIdType.MESH
 NT = (((1,), (1,)), ((), ()))
-CHUNKS = 2
+CHUNKS = 1
 PROGRAMS = {
-    0: (('s', 0, 0, 2), ('s', 0, 0, 1), ('s', 0, 1, 2), ('s', 0, 1, 1), ('w', 1, 0, -1), ('w', 1, 1, -1), ('w', 2, 0, -1), ('w', 2, 1, -1), ('w', 3, 0, -1), ('w', 4, 0, -1), ('w', 3, 1, -1), ('w', 4, 1, -1), ('w', 5, 0, -1), ('w', 6, 0, -1), ('w', 5, 1, -1), ('w', 6, 1, -1), ('w', 7, 0, -1), ('w', 7, 1, -1)),
-    1: (('s', 1, 0, 3), ('s', 1, 0, 2), ('s', 1, 0, 0), ('s', 1, 1, 3), ('s', 1, 1, 2), ('s', 1, 1, 0), ('w', 0, 0, -1), ('w', 2, 0, -1), ('w', 0, 1, -1), ('w', 2, 1, -1), ('w', 3, 0, -1), ('s', 3, 0, 0), ('w', 3, 1, -1), ('s', 3, 1, 0), ('w', 4, 0, -1), ('w', 5, 0, -1), ('s', 5, 0, 0), ('w', 4, 1, -1), ('w', 5, 1, -1), ('s', 5, 1, 0), ('w', 6, 0, -1), ('w', 7, 0, -1), ('s', 7, 0, 0), ('w', 6, 1, -1), ('w', 7, 1, -1), ('s', 7, 1, 0)),
-    2: (('s', 2, 0, 4), ('s', 2, 0, 0), ('s', 2, 0, 3), ('s', 2, 0, 1), ('s', 2, 1, 4), ('s', 2, 1, 0), ('s', 2, 1, 3), ('s', 2, 1, 1), ('w', 0, 0, -1), ('s', 0, 0, 4), ('s', 0, 0, 3), ('w', 3, 0, -1), ('w', 0, 1, -1), ('s', 0, 1, 4), ('s', 0, 1, 3), ('w', 3, 1, -1), ('w', 1, 0, -1), ('w', 4, 0, -1), ('s', 4, 0, 0), ('s', 4, 0, 1), ('w', 4, 1, -1), ('s', 4, 1, 0), ('s', 4, 1, 1), ('w', 1, 1, -1), ('w', 5, 0, -1), ('w', 6, 0, -1), ('s', 6, 0, 0), ('s', 6, 0, 1), ('w', 5, 1, -1), ('w', 6, 1, -1), ('s', 6, 1, 0), ('s', 6, 1, 1), ('w', 7, 0, -1), ('w', 7, 1, -1)),
-    3: (('s', 3, 0, 5), ('s', 3, 0, 1), ('s', 3, 0, 4), ('s', 3, 0, 2), ('s', 3, 1, 5), ('s', 3, 1, 1), ('s', 3, 1, 4), ('s', 3, 1, 2), ('w', 4, 0, -1), ('w', 4, 1, -1), ('w', 1, 0, -1), ('s', 1, 0, 5), ('s', 1, 0, 4), ('w', 5, 0, -1), ('s', 5, 0, 1), ('s', 5, 0, 2), ('w', 1, 1, -1), ('s', 1, 1, 5), ('s', 1, 1, 4), ('w', 5, 1, -1), ('s', 5, 1, 1), ('s', 5, 1, 2), ('w', 2, 0, -1), ('w', 2, 1, -1), ('w', 6, 0, -1), ('w', 0, 0, -1), ('w', 7, 0, -1), ('s', 7, 0, 1), ('s', 7, 0, 2), ('w', 6, 1, -1), ('w', 0, 1, -1), ('w', 7, 1, -1), ('s', 7, 1, 1), ('s', 7, 1, 2)),
-    4: (('s', 4, 0, 6), ('s', 4, 0, 2), ('s', 4, 0, 5), ('s', 4, 0, 3), ('s', 4, 1, 6), ('s', 4, 1, 2), ('s', 4, 1, 5), ('s', 4, 1, 3), ('w', 5, 0, -1), ('w', 5, 1, -1), ('w', 6, 0, -1), ('s', 6, 0, 2), ('s', 6, 0, 3), ('w', 6, 1, -1), ('s', 6, 1, 2), ('s', 6, 1, 3), ('w', 2, 0, -1), ('s', 2, 0, 6), ('s', 2, 0, 5), ('w', 2, 1, -1), ('s', 2, 1, 6), ('s', 2, 1, 5), ('w', 7, 0, -1), ('w', 3, 0, -1), ('w', 7, 1, -1), ('w', 3, 1, -1), ('w', 0, 0, -1), ('s', 0, 0, 6), ('s', 0, 0, 5), ('w', 0, 1, -1), ('s', 0, 1, 6), ('s', 0, 1, 5), ('w', 1, 0, -1), ('w', 1, 1, -1)),
-    5: (('s', 5, 0, 3), ('s', 5, 0, 7), ('s', 5, 0, 6), ('s', 5, 0, 4), ('s', 5, 1, 3), ('s', 5, 1, 7), ('s', 5, 1, 6), ('s', 5, 1, 4), ('w', 6, 0, -1), ('w', 6, 1, -1), ('w', 7, 0, -1), ('s', 7, 0, 3), ('s', 7, 0, 4), ('w', 7, 1, -1), ('s', 7, 1, 3), ('s', 7, 1, 4), ('w', 3, 0, -1), ('s', 3, 0, 7), ('s', 3, 0, 6), ('w', 3, 1, -1), ('s', 3, 1, 7), ('s', 3, 1, 6), ('w', 4, 0, -1), ('w', 4, 1, -1), ('w', 1, 0, -1), ('s', 1, 0, 7), ('s', 1, 0, 6), ('w', 1, 1, -1), ('s', 1, 1, 7), ('s', 1, 1, 6), ('w', 2, 0, -1), ('w', 2, 1, -1), ('w', 0, 0, -1), ('w', 0, 1, -1)),
-    6: (('s', 6, 0, 4), ('s', 6, 0, 7), ('s', 6, 0, 5), ('s', 6, 1, 4), ('s', 6, 1, 7), ('s', 6, 1, 5), ('w', 7, 0, -1), ('w', 7, 1, -1), ('w', 4, 0, -1), ('s', 4, 0, 7), ('w', 4, 1, -1), ('s', 4, 1, 7), ('w', 5, 0, -1), ('w', 5, 1, -1), ('w', 2, 0, -1), ('s', 2, 0, 7), ('w', 2, 1, -1), ('s', 2, 1, 7), ('w', 3, 0, -1), ('w', 3, 1, -1), ('w', 0, 0, -1), ('s', 0, 0, 7), ('w', 0, 1, -1), ('s', 0, 1, 7), ('w', 1, 0, -1), ('w', 1, 1, -1)),
-    7: (('s', 7, 0, 5), ('s', 7, 0, 6), ('s', 7, 1, 5), ('s', 7, 1, 6), ('w', 5, 0, -1), ('w', 5, 1, -1), ('w', 6, 0, -1), ('w', 6, 1, -1), ('w', 3, 0, -1), ('w', 3, 1, -1), ('w', 4, 0, -1), ('w', 4, 1, -1), ('w', 1, 0, -1), ('w', 1, 1, -1), ('w', 2, 0, -1), ('w', 2, 1, -1), ('w', 0, 0, -1), ('w', 0, 1, -1)),
+    0: (('s', 0, 0, 1), ('s', 0, 0, 3), ('w', 3, 0, -1), ('s', 3, 0, 1), ('w', 1, 0, -1), ('s', 3, 0, 2), ('w', 2, 0, -1), ('w', 4, 0, -1), ('w', 5, 0, -1), ('w', 6, 0, -1), ('w', 7, 0, -1)),
+    1: (('s', 1, 0, 4), ('s', 1, 0, 2), ('w', 0, 0, -1), ('s', 0, 0, 6), ('s', 1, 0, 6), ('s', 1, 0, 0), ('w', 2, 0, -1), ('s', 2, 0, 0), ('w', 4, 0, -1), ('s', 4, 0, 3), ('s', 4, 0, 2), ('s', 4, 0, 0), ('s', 0, 0, 2), ('w', 3, 0, -1), ('w', 7, 0, -1), ('s', 7, 0, 0), ('w', 6, 0, -1), ('w', 5, 0, -1)),
+    2: (('s', 2, 0, 5), ('s', 2, 0, 1), ('w', 1, 0, -1), ('s', 2, 0, 3), ('w', 5, 0, -1), ('s', 5, 0, 0), ('s', 5, 0, 3), ('s', 5, 0, 1), ('w', 6, 0, -1), ('w', 7, 0, -1), ('w', 4, 0, -1), ('w', 0, 0, -1), ('w', 3, 0, -1)),
+    3: (('s', 3, 0, 6), ('s', 3, 0, 0), ('w', 0, 0, -1), ('s', 0, 0, 5), ('s', 0, 0, 4), ('w', 6, 0, -1), ('s', 6, 0, 0), ('s', 6, 0, 4), ('s', 6, 0, 2), ('w', 2, 0, -1), ('w', 5, 0, -1), ('w', 1, 0, -1), ('w', 7, 0, -1), ('w', 4, 0, -1)),
+    4: (('s', 4, 0, 1), ('s', 4, 0, 7), ('w', 1, 0, -1), ('s', 1, 0, 7), ('s', 1, 0, 3), ('s', 1, 0, 5), ('w', 7, 0, -1), ('s', 7, 0, 2), ('s', 7, 0, 3), ('w', 5, 0, -1), ('w', 2, 0, -1), ('w', 0, 0, -1), ('w', 6, 0, -1), ('w', 3, 0, -1)),
+    5: (('s', 5, 0, 2), ('s', 5, 0, 6), ('w', 6, 0, -1), ('s', 5, 0, 4), ('w', 2, 0, -1), ('s', 2, 0, 7), ('s', 2, 0, 4), ('s', 2, 0, 6), ('w', 1, 0, -1), ('w', 0, 0, -1), ('w', 3, 0, -1), ('w', 7, 0, -1), ('w', 4, 0, -1)),
+    6: (('s', 6, 0, 3), ('s', 6, 0, 5), ('w', 7, 0, -1), ('s', 7, 0, 1), ('s', 6, 0, 1), ('s', 6, 0, 7), ('w', 5, 0, -1), ('s', 5, 0, 7), ('w', 3, 0, -1), ('s', 3, 0, 4), ('s', 3, 0, 5), ('s', 3, 0, 7), ('s', 7, 0, 5), ('w', 4, 0, -1), ('w', 0, 0, -1), ('s', 0, 0, 7), ('w', 1, 0, -1), ('w', 2, 0, -1)),
+    7: (('s', 7, 0, 6), ('s', 7, 0, 4), ('w', 4, 0, -1), ('s', 4, 0, 6), ('w', 6, 0, -1), ('s', 4, 0, 5), ('w', 5, 0, -1), ('w', 3, 0, -1), ('w', 2, 0, -1), ('w', 1, 0, -1), ('w', 0, 0, -1)),
 }
-PARTNERS = {0: (1, 2), 1: (0, 2, 3), 2: (0, 1, 3, 4), 3: (1, 2, 4, 5), 4: (2, 3, 5, 6), 5: (3, 4, 6, 7), 6: (4, 5, 7), 7: (5, 6)}
+PARTNERS = {0: (1, 2, 3), 1: (0, 2, 3, 4, 6), 2: (0, 1, 3, 4, 5), 3: (0, 1, 2, 4, 5, 6), 4: (1, 2, 3, 5, 6, 7), 5: (2, 3, 4, 6, 7), 6: (1, 3, 4, 5, 7), 7: (4, 5, 6)}
 
 
 def gelu(v):
@@ -33,7 +33,7 @@
     dims,
     list_hbm, count_hbm, feat_hbm, win_hbm, wh_hbm, blocks_hbm, ct_hbm,
     out_ref, grad_ref,
-    feat, win, blocks, z1, z2, ctb, ctp, wb, wct, gb, pb, rb, zb, zr,
+    feat, win, blocks, turned, z1, z2, ctb, ctp, wb, wct, gb, pb, rb, zb, zr,
     local_sem, line_send, line_recv, in_send, in_recv, ring_send, ring_recv,
     x_send, x_recv, z_send, z_recv, entered, lists, count,
 ):
@@ -64,6 +64,18 @@
             src_ref=src, dst_ref=dst, send_sem=send_sem, recv_sem=recv_sem,
             device_id=device, device_id_type=MESH,
         )
+
+    loads = [
+        pltpu.make_async_copy(feat_hbm, feat, local_sem.at[0]),
+        pltpu.make_async_copy(win_hbm, win, local_sem.at[1]),
+        pltpu.make_async_copy(ct_hbm, ctb.at[col], local_sem.at[2]),
+        pltpu.make_async_copy(wh_hbm, wb.at[col], local_sem.at[3]),
+        pltpu.make_async_copy(blocks_hbm, blocks, local_sem.at[4]),
+        pltpu.make_async_copy(list_hbm, lists, local_sem.at[5]),
+        pltpu.make_async_copy(count_hbm, count, local_sem.at[6]),
+    ]
+    for load in loads:
+        load.start()
 
     barrier = pltpu.get_barrier_semaphore()
     for steps, place in ((n_x, on_x), (n_col, on_col)):
@@ -84,18 +96,6 @@
             if v == n_dom - 1:
                 pl.semaphore_signal(barrier, inc=1, device_id=on_z(1), device_id_type=MESH)
 
-    loads = [
-        pltpu.make_async_copy(feat_hbm, feat, local_sem.at[0]),
-        pltpu.make_async_copy(win_hbm, win, local_sem.at[1]),
-        pltpu.make_async_copy(ct_hbm, ctb.at[col], local_sem.at[2]),
-        pltpu.make_async_copy(wh_hbm, wb.at[col], local_sem.at[3]),
-        pltpu.make_async_copy(blocks_hbm, blocks, local_sem.at[4]),
-        pltpu.make_async_copy(list_hbm, lists, local_sem.at[5]),
-        pltpu.make_async_copy(count_hbm, count, local_sem.at[6]),
-    ]
-    for load in loads:
-        load.start()
-
     def piece(buf, src, chunk):
         if CHUNKS == 1:
             return buf.at[2 * src : 2 * src + 2]
@@ -158,7 +158,7 @@
             first = jnp.where(used & (row == 0), 1.0, 0.0)
             second = jnp.where(used & (row == 1), 1.0, 0.0)
             both = jnp.concatenate([part * first, part * second], axis=0).astype(BF16)
-            total = total + lax.dot_general(both, blocks[slot], NT, preferred_element_type=F32)
+            total = total + jnp.dot(both, turned[slot], preferred_element_type=F32)
         return total
 
     loads[0].wait()
@@ -185,14 +185,20 @@
 
         lax.fori_loop(1, n_col, start, 0)
 
+    for load in loads[4:]:
+        load.wait()
+
+    def turn(slot, carry):
+        turned[slot] = blocks[slot].T
+        return carry
+
+    lax.fori_loop(0, 8, turn, 0)
     line_pass(0, z1)
 
     @pl.when(dom == n_dom - 1)
     def _():
         pl.semaphore_signal(entered, inc=1, device_id=on_z(1), device_id_type=MESH)
 
-    for load in loads[4:]:
-        load.wait()
     h1 = gelu(spread(z1)).astype(BF16)
     for j in range(2):
         for h in range(2):
@@ -245,7 +251,7 @@
     for copy in first:
         copy.start()
 
-    ga = gb[col].reshape(32, 1024)
+    ga = jnp.concatenate([g[:32], g[32:]], axis=1)
     part = lax.dot_general(ctp[...], ga, NT, preferred_element_type=F32)
     packed = jnp.concatenate([part[64 * q : 64 * q + 64] for q in range(4)], axis=1)
     for t in range(n_x):
@@ -331,6 +337,11 @@
         lax.fori_loop(1, n_col, done, 0)
     line_drain(0, z1)
     line_drain(1, z2)
+
+
+def hand_over(out_in, grad_in, out_ref, grad_ref):
+    out_ref[...] = out_in[...]
+    grad_ref[...] = grad_in[...]
 
 
 def solution(mesh):
@@ -354,6 +365,7 @@
             scratch_shapes=[
                 pltpu.VMEM((100, 1024), BF16),
                 pltpu.VMEM((32, 100), BF16),
+                pltpu.VMEM((8, 512, 512), BF16),
                 pltpu.VMEM((8, 512, 512), BF16),
                 pltpu.VMEM((2 * n_dom, 2, 16, 512), BF16),
                 pltpu.VMEM((2 * n_dom, 2, 16, 512), BF16),
@@ -391,6 +403,16 @@
             blocks[0, 0],
             cotangent[0].T,
         )
+        out, grad = pl.pallas_call(
+            hand_over,
+            out_shape=(
+                jax.ShapeDtypeStruct((32, 1024), BF16),
+                jax.ShapeDtypeStruct((4, 32), F32),
+            ),
+            in_specs=[vmem] * 2,
+            out_specs=(vmem, vmem),
+            compiler_params=pltpu.CompilerParams(vmem_limit_bytes=1024 * 1024),
+        )(out, grad)
         return out.T[None], grad.T
 
     return jax.shard_map(

time: 68.8 us -> 61.6 us (0.90)
  Pallas kernels: 63.8 us -> 58.4 us
  local copies, waits for them, and re-layouts: 2.72 us -> 1.5 us
    pallas_call x1, Pallas kernels: 63.8 us -> 57.8 us  [body(): pl.pallas_call(functools.partial(kernel, dims), out_shape=(jax.ShapeDtype...]
    unnamed x2 -> x4, local copies, waits for them, and re-layouts: 2.72 us -> 1.5 us
where the time goes in v3:
time: 61.6 us; the launch traced here: 61.2 us
  Pallas kernels  58.4 us (95%)
  local copies, waits for them, and re-layouts  1.5 us (2%)
  between operations  1.3 us (2%)
    pallas_call x1, Pallas kernels, body(): pl.pallas_call(functools.partial(kernel, dims), out_shape=(jax.ShapeDtype...  57.8 us
    unnamed x4, local copies, waits for them, and re-layouts  1.5 us

profile of v3, /device:TPU:24, one launch (start us, length us, event | category | flops | bytes accessed | tf_op | source)
XLA Modules:
  0.0 61.2 jit_solution(15938967694886114724)
XLA Ops:
  1.3 57.8 %shard_map.86 = (bf16[32,1024]{1,0:T(8,128)(2,1)}, f32[4,32]{1,0:T(4,128)}) custom-call(s32[1,3,1,8]{3,2,1,0:T(1,128)} %bitcast.17, s32[1,1]{1,0:T(1,128)S(6)} %copy.9.count_hbm, bf16[100,1024]{1,0:T(8,128)(2,1)} %bitcast.14, bf16[32,100]{1,0:T(8,128)(2,1)} %bitcast.16, bf16[32,256]{1,0:T(8,128)(2,1)} %wh_hbm.1, bf16[8,512,512]{2,1,0:T(8,128)(2,1)} %bitcast.13, ...), custom_call_target="tpu_custom_call" | custom-call | tf_op jit(solution)/shard_map/pallas_call | solution.py:357
  59.1 0.0 copy-start
  59.1 0.8 %copy-done = bf16[32,1024]{1,0:T(8,128)(2,1)S(1)} copy-done((bf16[32,1024]{1,0:T(8,128)(2,1)S(1)}, bf16[32,1024]{1,0:T(8,128)(2,1)}, u32[]{:S(2)}) %copy-start) | copy-done | bytes 65560
  59.9 0.0 copy-start.1
  59.9 0.7 %copy-done.1 = f32[4,32]{1,0:T(4,128)S(1)} copy-done((f32[4,32]{1,0:T(4,128)S(1)}, f32[4,32]{1,0:T(4,128)}, u32[]{:S(2)}) %copy-start.1) | copy-done | bytes 536
  60.6 0.6 %shard_map.87 = (bf16[32,1024]{1,0:T(8,128)(2,1)}, f32[4,32]{1,0:T(4,128)}) custom-call(bf16[32,1024]{1,0:T(8,128)(2,1)S(1)} %copy-done, f32[4,32]{1,0:T(4,128)S(1)} %copy-done.1), custom_call_target="tpu_custom_call" | custom-call | tf_op jit(solution)/shard_map/pallas_call | solution.py:406
Async XLA Ops:
  59.1 0.8 %copy-start = (bf16[32,1024]{1,0:T(8,128)(2,1)S(1)}, bf16[32,1024]{1,0:T(8,128)(2,1)}, u32[]{:S(2)}) copy-start(bf16[32,1024]{1,0:T(8,128)(2,1)} %get-tuple-element.6.out_in) | copy-start | bytes 196612
  59.9 0.7 %copy-start.1 = (f32[4,32]{1,0:T(4,128)S(1)}, f32[4,32]{1,0:T(4,128)}, u32[]{:S(2)}) copy-start(f32[4,32]{1,0:T(4,128)} %get-tuple-element.7.grad_in) | copy-start | bytes 1540

commit v4 on v3

--- a/solution.py
+++ b/solution.py
@@ -91,10 +91,14 @@
                 pl.semaphore_signal(
                     barrier, inc=1, device_id={"dom": partner}, device_id_type=MESH
                 )
-            if v == 0:
-                pl.semaphore_signal(barrier, inc=1, device_id=on_z(n_z - 1), device_id_type=MESH)
-            if v == n_dom - 1:
-                pl.semaphore_signal(barrier, inc=1, device_id=on_z(1), device_id_type=MESH)
+
+    @pl.when(dom == 0)
+    def _():
+        pl.semaphore_signal(barrier, inc=1, device_id=on_z(n_z - 1), device_id_type=MESH)
+
+    @pl.when(dom == n_dom - 1)
+    def _():
+        pl.semaphore_signal(barrier, inc=1, device_id=on_z(1), device_id_type=MESH)
 
     def piece(buf, src, chunk):
         if CHUNKS == 1:
@@ -248,9 +252,9 @@
         ring_copy(2, col, 1, up), ring_copy(3, col, 0, down),
         ring_copy(4, col, None, sibling),
     ]
+
     for copy in first:
         copy.start()
-
     ga = jnp.concatenate([g[:32], g[32:]], axis=1)
     part = lax.dot_general(ctp[...], ga, NT, preferred_element_type=F32)
     packed = jnp.concatenate([part[64 * q : 64 * q + 64] for q in range(4)], axis=1)
@@ -311,24 +315,11 @@
         wct[...], gb[...].reshape(256, 1024), preferred_element_type=F32
     ).astype(BF16)
 
-    def z_add(step, total):
-        z_copy(step).wait_recv()
-        return total + zr[step]
-
-    total = lax.fori_loop(1, n_z, z_add, zb[z])
-    for q in range(4):
-        grad_ref[q : q + 1, :] = total[:, 32 * q : 32 * q + 32]
-
     for copy in first + second + third:
         copy.wait_send()
     for step in range(1, n_x):
         x_copy(step).wait_send()
 
-    def z_done(step, carry):
-        z_copy(step).wait_send()
-        return carry
-
-    lax.fori_loop(1, n_z, z_done, 0)
     for a, buf in ((0, wb), (1, ctb)):
         def done(step, carry, a=a, buf=buf):
             gather_copy(a, buf, step).wait_send()
@@ -338,10 +329,30 @@
     line_drain(0, z1)
     line_drain(1, z2)
 
-
-def hand_over(out_in, grad_in, out_ref, grad_ref):
-    out_ref[...] = out_in[...]
-    grad_ref[...] = grad_in[...]
+    def z_add(step, total):
+        z_copy(step).wait_recv()
+        return total + zr[step]
+
+    total = lax.fori_loop(1, n_z, z_add, zb[z])
+    for q in range(4):
+        grad_ref[q : q + 1, :] = total[:, 32 * q : 32 * q + 32]
+
+    def z_done(step, carry):
+        z_copy(step).wait_send()
+        return carry
+
+    lax.fori_loop(1, n_z, z_done, 0)
+
+
+def hand_over(out_held, grad_held, out_ref, grad_ref, sems):
+    copies = [
+        pltpu.make_async_copy(out_held, out_ref, sems.at[0]),
+        pltpu.make_async_copy(grad_held, grad_ref, sems.at[1]),
+    ]
+    for copy in copies:
+        copy.start()
+    for copy in copies:
+        copy.wait()
 
 
 def solution(mesh):
@@ -357,8 +368,8 @@
         out, grad = pl.pallas_call(
             functools.partial(kernel, dims),
             out_shape=(
-                jax.ShapeDtypeStruct((32, 1024), BF16),
-                jax.ShapeDtypeStruct((4, 32), F32),
+                pltpu.VMEM((32, 1024), BF16),
+                pltpu.VMEM((4, 32), F32),
             ),
             in_specs=[hbm] * 7,
             out_specs=(vmem, vmem),
@@ -410,7 +421,8 @@
                 jax.ShapeDtypeStruct((4, 32), F32),
             ),
             in_specs=[vmem] * 2,
-            out_specs=(vmem, vmem),
+            out_specs=(hbm, hbm),
+            scratch_shapes=[dma((2,))],
             compiler_params=pltpu.CompilerParams(vmem_limit_bytes=1024 * 1024),
         )(out, grad)
         return out.T[None], grad.T

time: 61.6 us -> 59.2 us (0.961)
  local copies, waits for them, and re-layouts: 1.5 us -> 0 us
  Pallas kernels: 58.4 us -> 57.5 us
    unnamed x4 -> x0, local copies, waits for them, and re-layouts: 1.5 us -> none
    pallas_call x1, Pallas kernels: 57.8 us -> 56.9 us  [body(): pl.pallas_call(functools.partial(kernel, dims), out_shape=(pltpu.VMEM((32...]
where the time goes in v4:
time: 59.2 us; the launch traced here: 58.8 us
  Pallas kernels  57.5 us (97%)
  between operations  1.29 us (2%)
    pallas_call x1, Pallas kernels, body(): pl.pallas_call(functools.partial(kernel, dims), out_shape=(pltpu.VMEM((32...  56.9 us

profile of v4, /device:TPU:24, one launch (start us, length us, event | category | flops | bytes accessed | tf_op | source)
XLA Modules:
  0.0 58.8 jit_solution(4311869612632259161)
XLA Ops:
  1.3 56.9 %shard_map.86 = (bf16[32,1024]{1,0:T(8,128)(2,1)S(1)}, f32[4,32]{1,0:T(4,128)S(1)}) custom-call(s32[1,3,1,8]{3,2,1,0:T(1,128)} %bitcast.17, s32[1,1]{1,0:T(1,128)S(6)} %copy.9.count_hbm, bf16[100,1024]{1,0:T(8,128)(2,1)} %bitcast.14, bf16[32,100]{1,0:T(8,128)(2,1)} %bitcast.16, bf16[32,256]{1,0:T(8,128)(2,1)} %wh_hbm.1, bf16[8,512,512]{2,1,0:T(8,128)(2,1)} %bitcast.13, ...), custom_call_target="tpu_custom_call" | custom-call | tf_op jit(solution)/shard_map/pallas_call | solution.py:368
  58.2 0.7 %shard_map.87 = (bf16[32,1024]{1,0:T(8,128)(2,1)}, f32[4,32]{1,0:T(4,128)}) custom-call(bf16[32,1024]{1,0:T(8,128)(2,1)S(1)} %get-tuple-element.6.out_held, f32[4,32]{1,0:T(4,128)S(1)} %get-tuple-element.7.grad_held), custom_call_target="tpu_custom_call" | custom-call | tf_op jit(solution)/shard_map/pallas_call | solution.py:417

commit v5 on v4

--- a/solution.py
+++ b/solution.py
@@ -13,14 +13,14 @@
 NT = (((1,), (1,)), ((), ()))
 CHUNKS = 1
 PROGRAMS = {
-    0: (('s', 0, 0, 1), ('s', 0, 0, 3), ('w', 3, 0, -1), ('s', 3, 0, 1), ('w', 1, 0, -1), ('s', 3, 0, 2), ('w', 2, 0, -1), ('w', 4, 0, -1), ('w', 5, 0, -1), ('w', 6, 0, -1), ('w', 7, 0, -1)),
-    1: (('s', 1, 0, 4), ('s', 1, 0, 2), ('w', 0, 0, -1), ('s', 0, 0, 6), ('s', 1, 0, 6), ('s', 1, 0, 0), ('w', 2, 0, -1), ('s', 2, 0, 0), ('w', 4, 0, -1), ('s', 4, 0, 3), ('s', 4, 0, 2), ('s', 4, 0, 0), ('s', 0, 0, 2), ('w', 3, 0, -1), ('w', 7, 0, -1), ('s', 7, 0, 0), ('w', 6, 0, -1), ('w', 5, 0, -1)),
-    2: (('s', 2, 0, 5), ('s', 2, 0, 1), ('w', 1, 0, -1), ('s', 2, 0, 3), ('w', 5, 0, -1), ('s', 5, 0, 0), ('s', 5, 0, 3), ('s', 5, 0, 1), ('w', 6, 0, -1), ('w', 7, 0, -1), ('w', 4, 0, -1), ('w', 0, 0, -1), ('w', 3, 0, -1)),
-    3: (('s', 3, 0, 6), ('s', 3, 0, 0), ('w', 0, 0, -1), ('s', 0, 0, 5), ('s', 0, 0, 4), ('w', 6, 0, -1), ('s', 6, 0, 0), ('s', 6, 0, 4), ('s', 6, 0, 2), ('w', 2, 0, -1), ('w', 5, 0, -1), ('w', 1, 0, -1), ('w', 7, 0, -1), ('w', 4, 0, -1)),
-    4: (('s', 4, 0, 1), ('s', 4, 0, 7), ('w', 1, 0, -1), ('s', 1, 0, 7), ('s', 1, 0, 3), ('s', 1, 0, 5), ('w', 7, 0, -1), ('s', 7, 0, 2), ('s', 7, 0, 3), ('w', 5, 0, -1), ('w', 2, 0, -1), ('w', 0, 0, -1), ('w', 6, 0, -1), ('w', 3, 0, -1)),
-    5: (('s', 5, 0, 2), ('s', 5, 0, 6), ('w', 6, 0, -1), ('s', 5, 0, 4), ('w', 2, 0, -1), ('s', 2, 0, 7), ('s', 2, 0, 4), ('s', 2, 0, 6), ('w', 1, 0, -1), ('w', 0, 0, -1), ('w', 3, 0, -1), ('w', 7, 0, -1), ('w', 4, 0, -1)),
-    6: (('s', 6, 0, 3), ('s', 6, 0, 5), ('w', 7, 0, -1), ('s', 7, 0, 1), ('s', 6, 0, 1), ('s', 6, 0, 7), ('w', 5, 0, -1), ('s', 5, 0, 7), ('w', 3, 0, -1), ('s', 3, 0, 4), ('s', 3, 0, 5), ('s', 3, 0, 7), ('s', 7, 0, 5), ('w', 4, 0, -1), ('w', 0, 0, -1), ('s', 0, 0, 7), ('w', 1, 0, -1), ('w', 2, 0, -1)),
-    7: (('s', 7, 0, 6), ('s', 7, 0, 4), ('w', 4, 0, -1), ('s', 4, 0, 6), ('w', 6, 0, -1), ('s', 4, 0, 5), ('w', 5, 0, -1), ('w', 3, 0, -1), ('w', 2, 0, -1), ('w', 1, 0, -1), ('w', 0, 0, -1)),
+    0: (('s', 0, 0, 1), ('s', 0, 0, 3), ('w', 3, 0, -1), ('s', 3, 0, 1), ('w', 1, 0, -1), ('s', 3, 0, 2), ('w', 2, 0, -1), ('w', 4, 0, -1), ('w', 5, 0, -1), ('w', 7, 0, -1), ('w', 6, 0, -1)),
+    1: (('s', 1, 0, 4), ('s', 1, 0, 2), ('w', 0, 0, -1), ('s', 0, 0, 6), ('s', 1, 0, 0), ('w', 2, 0, -1), ('s', 2, 0, 0), ('w', 4, 0, -1), ('s', 4, 0, 3), ('s', 4, 0, 2), ('s', 4, 0, 0), ('s', 0, 0, 2), ('w', 7, 0, -1), ('s', 7, 0, 0), ('w', 3, 0, -1), ('w', 5, 0, -1), ('w', 6, 0, -1)),
+    2: (('s', 2, 0, 5), ('s', 2, 0, 1), ('w', 1, 0, -1), ('s', 2, 0, 3), ('w', 5, 0, -1), ('s', 5, 0, 0), ('s', 5, 0, 3), ('s', 5, 0, 1), ('w', 4, 0, -1), ('w', 0, 0, -1), ('w', 6, 0, -1), ('w', 7, 0, -1), ('w', 3, 0, -1)),
+    3: (('s', 3, 0, 6), ('s', 3, 0, 0), ('w', 0, 0, -1), ('s', 0, 0, 5), ('s', 0, 0, 4), ('w', 6, 0, -1), ('s', 6, 0, 0), ('s', 6, 0, 1), ('s', 6, 0, 4), ('s', 6, 0, 2), ('w', 2, 0, -1), ('w', 5, 0, -1), ('w', 1, 0, -1), ('w', 7, 0, -1), ('w', 4, 0, -1)),
+    4: (('s', 4, 0, 1), ('s', 4, 0, 7), ('w', 1, 0, -1), ('s', 1, 0, 7), ('s', 1, 0, 6), ('s', 1, 0, 3), ('s', 1, 0, 5), ('w', 7, 0, -1), ('s', 7, 0, 2), ('s', 7, 0, 3), ('w', 5, 0, -1), ('w', 2, 0, -1), ('w', 0, 0, -1), ('w', 6, 0, -1), ('w', 3, 0, -1)),
+    5: (('s', 5, 0, 2), ('s', 5, 0, 6), ('w', 6, 0, -1), ('s', 5, 0, 4), ('w', 2, 0, -1), ('s', 2, 0, 7), ('s', 2, 0, 4), ('s', 2, 0, 6), ('w', 3, 0, -1), ('w', 7, 0, -1), ('w', 1, 0, -1), ('w', 0, 0, -1), ('w', 4, 0, -1)),
+    6: (('s', 6, 0, 3), ('s', 6, 0, 5), ('w', 7, 0, -1), ('s', 7, 0, 1), ('s', 6, 0, 7), ('w', 5, 0, -1), ('s', 5, 0, 7), ('w', 3, 0, -1), ('s', 3, 0, 4), ('s', 3, 0, 5), ('s', 3, 0, 7), ('s', 7, 0, 5), ('w', 0, 0, -1), ('s', 0, 0, 7), ('w', 4, 0, -1), ('w', 2, 0, -1), ('w', 1, 0, -1)),
+    7: (('s', 7, 0, 6), ('s', 7, 0, 4), ('w', 4, 0, -1), ('s', 4, 0, 6), ('w', 6, 0, -1), ('s', 4, 0, 5), ('w', 5, 0, -1), ('w', 3, 0, -1), ('w', 2, 0, -1), ('w', 0, 0, -1), ('w', 1, 0, -1)),
 }
 PARTNERS = {0: (1, 2, 3), 1: (0, 2, 3, 4, 6), 2: (0, 1, 3, 4, 5), 3: (0, 1, 2, 4, 5, 6), 4: (1, 2, 3, 5, 6, 7), 5: (2, 3, 4, 6, 7), 6: (1, 3, 4, 5, 7), 7: (4, 5, 6)}
 
@@ -158,10 +158,12 @@
         for slot in range(8):
             used = slot < count[0, 0]
             row = lists[0, 0, 0, slot]
-            part = buf[2 * lists[0, 1, 0, slot] + lists[0, 2, 0, slot]].reshape(32, 512).astype(F32)
+            part = buf[2 * lists[0, 1, 0, slot] + lists[0, 2, 0, slot]].reshape(32, 512)
             first = jnp.where(used & (row == 0), 1.0, 0.0)
             second = jnp.where(used & (row == 1), 1.0, 0.0)
-            both = jnp.concatenate([part * first, part * second], axis=0).astype(BF16)
+            first = jnp.full((32, 512), first, F32).astype(BF16)
+            second = jnp.full((32, 512), second, F32).astype(BF16)
+            both = jnp.concatenate([part * first, part * second], axis=0)
             total = total + jnp.dot(both, turned[slot], preferred_element_type=F32)
         return total
 

time: 59.2 us -> 58.5 us (0.988)
  no operation moved by 1% of the time
where the time goes in v5:
time: 58.5 us; the launch traced here: 58.4 us
  Pallas kernels  57.1 us (98%)
  between operations  1.29 us (2%)
    pallas_call x1, Pallas kernels, body(): pl.pallas_call(functools.partial(kernel, dims), out_shape=(pltpu.VMEM((32...  56.5 us

profile of v5, /device:TPU:24, one launch (start us, length us, event | category | flops | bytes accessed | tf_op | source)
XLA Modules:
  0.0 58.4 jit_solution(15561584099231698628)
XLA Ops:
  1.3 56.5 %shard_map.86 = (bf16[32,1024]{1,0:T(8,128)(2,1)S(1)}, f32[4,32]{1,0:T(4,128)S(1)}) custom-call(s32[1,3,1,8]{3,2,1,0:T(1,128)} %bitcast.17, s32[1,1]{1,0:T(1,128)S(6)} %copy.9.count_hbm, bf16[100,1024]{1,0:T(8,128)(2,1)} %bitcast.14, bf16[32,100]{1,0:T(8,128)(2,1)} %bitcast.16, bf16[32,256]{1,0:T(8,128)(2,1)} %wh_hbm.1, bf16[8,512,512]{2,1,0:T(8,128)(2,1)} %bitcast.13, ...), custom_call_target="tpu_custom_call" | custom-call | tf_op jit(solution)/shard_map/pallas_call | solution.py:370
  57.7 0.7 %shard_map.87 = (bf16[32,1024]{1,0:T(8,128)(2,1)}, f32[4,32]{1,0:T(4,128)}) custom-call(bf16[32,1024]{1,0:T(8,128)(2,1)S(1)} %get-tuple-element.6.out_held, f32[4,32]{1,0:T(4,128)S(1)} %get-tuple-element.7.grad_held), custom_call_target="tpu_custom_call" | custom-call | tf_op jit(solution)/shard_map/pallas_call | solution.py:419
